TPU v7x, 256 devices: a whole 4x4x8 slice. The times are simulated.
256 devices in a mesh: section: 8 (over y, x_lo), dp: 32 (over x_hi, z, core).
Axes of the slice: x: 4 (x_hi: 2, x_lo: 2; x = x_hi * 2 + x_lo), y: 4, z: 8, core: 2. Of those that a mesh axis runs over, the one named last changes fastest.
Arguments:
- inputs: bfloat16 [8, 2, 2048, 4096], P('section', None, 'dp'), may hold values from -6 to 6
- cotangent: bfloat16 [2, 2048, 4096], P(None, 'dp'), may hold values from -6 to 6
- norm_gain: bfloat16 [8, 4096], P('section', 'dp'), may hold values from 0.5 to 1.5
- key_weight: bfloat16 [8, 4096, 512], P('section', 'dp'), may hold values from -0.09375 to 0.09375
- value_weight: bfloat16 [8, 4096, 512], P('section', 'dp'), may hold values from -0.09375 to 0.09375
- plan: int32 [8, 2], P('section'), may hold values from 0 to 1, each once within a row
Outputs:
- grad_inputs: bfloat16 [8, 2, 2048, 4096], P('section', None, 'dp')
- key_weight_grad: float32 [8, 4096, 512], P('section', 'dp')
- value_weight_grad: float32 [8, 4096, 512], P('section', 'dp')
- gain_grad: float32 [8, 4096], P('section', 'dp')
Inputs may be any that keep to these rules, and one draw needn't show every extreme that they name: Each row of plan lists every micro-batch once.
All inputs are finite; a program needn't handle non-finite values.
Results may differ from a plain program's by a relative error of at most 0.03.
Values may be sent and summed in bfloat16 or wider, within the bound.
A program may use at most 128 MiB of HBM per device.

v0:
```python
import math

import jax
import jax.numpy as jnp
from jax import lax
from jax.sharding import Mesh
from jax.sharding import PartitionSpec as P

HEADS = 32
KV_HEADS = 4
HEAD_DIM = 128
GROUP = 8
DP = ("dp_0", "dp_1", "dp_2")


eps = 1e-05
rope_base = 500000.0


def in_order(parts, dim):
    dims = list(parts.shape[1:])
    dims[dim] *= parts.shape[0]
    return jnp.moveaxis(parts, 0, dim).reshape(dims)


def gather_in_order(value, axes, order):
    parts = value
    for k in order:
        parts = lax.all_gather(parts, axes[k])
    done = order[::-1]
    back = [done.index(k) for k in range(len(axes))]
    parts = parts.transpose(*back, *range(len(axes), parts.ndim))
    return parts.reshape(-1, *value.shape)


def gathered_by_axis(value, axes, order, dim):
    return in_order(gather_in_order(value, axes, order), dim)


def from_behind(value, axis, steps):
    count = lax.axis_size(axis)
    first, last = (max(0, -steps), min(count, count - steps))
    return lax.ppermute(value, axis, [(source, source + steps) for source in range(first, last)])


def side_by_side(arrays, axis, dim, along):
    columns = [a.reshape(*a.shape[:along], -1) for a in arrays]
    both = jnp.concatenate(columns, axis=along)
    whole, at, gathered = (lax.psum_scatter(both, axis, scatter_dimension=dim, tiled=True), 0, [])
    for a, column in zip(arrays, columns):
        section = whole[..., at : at + column.shape[along]]
        gathered.append(section.reshape(*section.shape[:along], *a.shape[along:]))
        at += column.shape[along]
    return tuple(gathered)


def rope_tables(length, head_dim):
    half_dim = head_dim // 2
    frequency = rope_base ** (-(jnp.arange(half_dim, dtype=jnp.float32) * 2.0 / head_dim))
    angles = jnp.arange(length, dtype=jnp.float32)[:, None] * frequency[None, :]
    cosine = jnp.concatenate([jnp.cos(angles), jnp.cos(angles)], axis=-1)
    sine_tab = jnp.concatenate([jnp.sin(angles), jnp.sin(angles)], axis=-1)
    return (cosine[:, None, :], sine_tab[:, None, :])


def turned(values):
    half_dim = values.shape[-1] // 2
    return jnp.concatenate([-values[..., half_dim:], values[..., :half_dim]], axis=-1)


def rotate(values, cosine, sine_tab):
    return values * cosine + turned(values) * sine_tab


def unrotate(values, cosine, sine_tab):
    return values * cosine - turned(values) * sine_tab


def contract_rows(left, right):
    return lax.dot_general(
        left, right, (((0,), (0,)), ((), ())), preferred_element_type=jnp.float32
    )


def contract_cols(left, right):
    return lax.dot_general(
        left, right, (((1,), (1,)), ((), ())), preferred_element_type=jnp.float32
    )


def body(inputs, cotangent, norm_gain, key_weight, value_weight, plan):
    sections = lax.axis_size("section")
    section_index = lax.axis_index("section")
    batches = inputs.shape[1]
    local_tok = inputs.shape[2]
    model_width = inputs.shape[3]
    kv_width = key_weight.shape[2]
    head_dim = HEAD_DIM
    key_heads = KV_HEADS
    query_heads = HEADS
    group_count = GROUP
    score_scale = 1.0 / math.sqrt(head_dim)
    all_rows = batches * local_tok
    widened = inputs[0].reshape(all_rows, model_width).astype(jnp.float32)
    inv_rms = lax.rsqrt(jnp.mean(widened * widened, axis=-1, keepdims=True) + eps)
    full_key, full_value, full_gain = (
        gathered_by_axis(key_weight[0], DP, (0, 1, 2), 0),
        gathered_by_axis(value_weight[0], DP, (0, 1, 2), 0),
        gathered_by_axis(norm_gain[0], DP, (0, 1, 2), 0),
    )
    gain_full = full_gain.astype(jnp.float32)
    normed = (widened * inv_rms * gain_full).astype(jnp.bfloat16)
    key_pre = jnp.dot(normed, full_key, preferred_element_type=jnp.float32)
    value_pre = jnp.dot(normed, full_value, preferred_element_type=jnp.float32)
    cosine, sine_tab = rope_tables(local_tok, head_dim)
    key_rot = rotate(
        key_pre.reshape(batches, local_tok, key_heads, head_dim), cosine, sine_tab
    ).astype(jnp.bfloat16)
    value_heads = value_pre.astype(jnp.bfloat16).reshape(batches, local_tok, key_heads, head_dim)
    query_rot = rotate(
        normed.astype(jnp.float32).reshape(batches, local_tok, query_heads, head_dim),
        cosine,
        sine_tab,
    ).astype(jnp.bfloat16)
    query_rot = query_rot.reshape(batches, local_tok, key_heads, group_count, head_dim)
    scores = (
        jnp.einsum("blkgd,bmkd->bkglm", query_rot, key_rot, preferred_element_type=jnp.float32)
        * score_scale
    )
    causal = jnp.arange(local_tok)[:, None] >= jnp.arange(local_tok)[None, :]
    raised = jnp.where(causal, jnp.exp(scores), 0.0)
    attn_prob = raised / jnp.sum(raised, axis=-1, keepdims=True)
    prob_low = attn_prob.astype(jnp.bfloat16)

    def busy_turn(operands):
        slot_index, incoming, stores = operands
        lower_store, key_store, value_store, sum_gain, sum_key, sum_value = stores
        first_row = slot_index * local_tok
        own_cotangent = lax.dynamic_index_in_dim(cotangent, slot_index, 0, keepdims=False)
        upper_grad = jnp.where(section_index == sections - 1, own_cotangent, incoming)
        part_wide = lax.dynamic_slice_in_dim(widened, first_row, local_tok, 0)
        part_inv = lax.dynamic_slice_in_dim(inv_rms, first_row, local_tok, 0)
        part_query = lax.dynamic_index_in_dim(query_rot, slot_index, 0, keepdims=False)
        part_key = lax.dynamic_index_in_dim(key_rot, slot_index, 0, keepdims=False)
        part_value = lax.dynamic_index_in_dim(value_heads, slot_index, 0, keepdims=False)
        part_prob = lax.dynamic_index_in_dim(attn_prob, slot_index, 0, keepdims=False)
        part_low = lax.dynamic_index_in_dim(prob_low, slot_index, 0, keepdims=False)
        grad_heads = upper_grad.reshape(local_tok, key_heads, group_count, head_dim)
        grad_prob = jnp.einsum(
            "lkgd,mkd->kglm", grad_heads, part_value, preferred_element_type=jnp.float32
        )
        grad_value = jnp.einsum(
            "kglm,lkgd->mkd", part_low, grad_heads, preferred_element_type=jnp.float32
        ).astype(jnp.bfloat16)
        row_dot = jnp.sum(part_prob * grad_prob, axis=-1, keepdims=True)
        grad_score = (part_prob * (grad_prob - row_dot) * score_scale).astype(jnp.bfloat16)
        grad_query = jnp.einsum(
            "kglm,mkd->lkgd", grad_score, part_key, preferred_element_type=jnp.float32
        )
        grad_key = jnp.einsum(
            "kglm,lkgd->mkd", grad_score, part_query, preferred_element_type=jnp.float32
        )
        query_back = unrotate(
            grad_query.reshape(local_tok, query_heads, head_dim), cosine, sine_tab
        ).reshape(local_tok, model_width)
        key_back = (
            unrotate(grad_key, cosine, sine_tab).astype(jnp.bfloat16).reshape(local_tok, kv_width)
        )
        value_flat = grad_value.reshape(local_tok, kv_width)
        grad_normed = query_back + (
            contract_cols(key_back, full_key) + contract_cols(value_flat, full_value)
        )
        gain_term = grad_normed * part_wide * part_inv
        projected = jnp.mean(gain_term * gain_full, axis=-1, keepdims=True)
        lower_grad = (
            upper_grad.astype(jnp.float32)
            + part_inv * gain_full * grad_normed
            - part_wide * part_inv * part_inv * projected
        )
        lower_grad = lower_grad.astype(jnp.bfloat16)
        lower_store = lax.dynamic_update_index_in_dim(lower_store, lower_grad, slot_index, 0)
        key_store = lax.dynamic_update_slice_in_dim(key_store, key_back, first_row, 0)
        value_store = lax.dynamic_update_slice_in_dim(value_store, value_flat, first_row, 0)
        sum_gain = sum_gain + jnp.sum(gain_term, axis=0)
        return (lower_grad, (lower_store, key_store, value_store, sum_gain, sum_key, sum_value))

    def quiet_turn(operands):
        return (jnp.zeros((local_tok, model_width), jnp.bfloat16), operands[2])

    def one_turn(turn_index, carried):
        incoming, stores = carried
        slot_index = turn_index - (sections - 1 - section_index)
        active = (slot_index >= 0) & (slot_index < batches)
        clipped = jnp.clip(slot_index, 0, batches - 1)
        lower_grad, stores = lax.cond(active, busy_turn, quiet_turn, (clipped, incoming, stores))
        incoming = from_behind(lower_grad, "section", -1)
        return (incoming, stores)

    stores = (
        jnp.zeros((batches, local_tok, model_width), jnp.bfloat16),
        jnp.zeros((all_rows, kv_width), jnp.bfloat16),
        jnp.zeros((all_rows, kv_width), jnp.bfloat16),
        jnp.zeros((model_width,), jnp.float32),
        jnp.zeros((model_width, kv_width), jnp.float32),
        jnp.zeros((model_width, kv_width), jnp.float32),
    )
    incoming = jnp.zeros((local_tok, model_width), jnp.bfloat16)
    incoming, stores = lax.fori_loop(0, sections - 1 + batches, one_turn, (incoming, stores))
    lower_store, key_store, value_store, sum_gain, sum_key, sum_value = stores
    sum_key = contract_rows(normed, key_store)
    sum_value = contract_rows(normed, value_store)
    summed = tuple(
        (
            part.astype(jnp.float32)
            for part in side_by_side(
                (
                    sum_key.astype(jnp.bfloat16),
                    sum_value.astype(jnp.bfloat16),
                    sum_gain.astype(jnp.bfloat16),
                ),
                DP,
                0,
                1,
            )
        )
    )
    selector = plan[0][:, None] == jnp.arange(batches, dtype=jnp.int32)[None, :]
    ordered = jnp.sum(
        jnp.where(selector[:, :, None, None], lower_store[None], jnp.zeros((), jnp.bfloat16)),
        axis=1,
    )
    return (ordered[None], summed[0][None], summed[1][None], summed[2][None])


def solution(mesh):
    split = Mesh(
        mesh.devices.reshape(mesh.shape["section"], 2, 8, 2), ("section", "dp_0", "dp_1", "dp_2")
    )
    placed = (
        P("section", None, DP, None),
        P(None, DP, None),
        P("section", DP),
        P("section", DP, None),
        P("section", DP, None),
        P("section", None),
    )
    return jax.shard_map(
        body,
        mesh=split,
        in_specs=placed,
        out_specs=(
            P("section", None, DP, None),
            P("section", DP, None),
            P("section", DP, None),
            P("section", DP),
        ),
        check_vma=False,
    )
```

profile of v0, /device:TPU:1, one launch (start us, length us, event | category | flops | bytes accessed | tf_op | source)
XLA Modules:
  0.0 694.7 jit_solution(5636349398373317497)
XLA Ops:
  7.2 8.5 %all_gather.50 = bf16[2,128,512]{2,1,0:T(8,128)(2,1)} all-gather(bf16[1,128,512]{2,1,0:T(8,128)(2,1)} %param.13), channel_id=1, replica_groups=mesh['section'=8,'dp_0'=2,'dp_1'=8,'dp_2'=2] {'dp_0'}, dimensions={0}, use_global_device_ids=true | all-gather | bytes 393216 | tf_op jit(solution)/shard_map/all_gather | solution.py:29
  15.8 6.7 all_gather.55
  22.6 33.1 %all-gather.13.cloned.1.call-done = bf16[16,128,512]{2,1,0:T(8,128)(2,1)} async-done(((bf16[2,128,512]{2,1,0:T(8,128)(2,1)}), bf16[16,128,512]{2,1,0:T(8,128)(2,1)}) %all-gather.13.cloned.1.call-update) | async-done | bytes 2097168 | tf_op jit(solution)/shard_map/all_gather | solution.py:29
  61.9 11.3 %all-gather.7 = bf16[8,2,128]{2,1,0:T(2,128)(2,1)S(1)} all-gather(bf16[1,2,128]{2,1,0:T(2,128)(2,1)S(1)} %bitcast.265), channel_id=2, replica_groups=mesh['section'=8,'dp_0'=2,'dp_1'=8,'dp_2'=2] {'dp_1'}, dimensions={0}, use_global_device_ids=true | all-gather | bytes 4608 | tf_op jit(solution)/shard_map/all_gather | solution.py:29
  73.2 11.5 %all-gather.1 = bf16[16,2,128]{2,1,0:T(2,128)(2,1)S(1)} all-gather(bf16[8,2,128]{2,1,0:T(2,128)(2,1)S(1)} %all-gather.7), channel_id=3, replica_groups=mesh['section'=8,'dp_0'=2,'dp_1'=8,'dp_2'=2] {'dp_2'}, dimensions={0}, use_global_device_ids=true | all-gather | bytes 12288 | tf_op jit(solution)/shard_map/all_gather | solution.py:29
  87.3 9.6 %all-gather.17.cloned.1.call-done = bf16[16,128,512]{2,1,0:T(8,128)(2,1)} async-done(((bf16[2,128,512]{2,1,0:T(8,128)(2,1)}), bf16[16,128,512]{2,1,0:T(8,128)(2,1)}) %all-gather.17.cloned.1.call-update) | async-done | bytes 2097168 | tf_op jit(solution)/shard_map/all_gather | solution.py:29
  102.9 18.4 %all-gather.15.cloned.1.call-done = bf16[16,2,128,512]{3,2,1,0:T(8,128)(2,1)} async-done(((bf16[8,2,128,512]{3,2,1,0:T(8,128)(2,1)}), bf16[16,2,128,512]{3,2,1,0:T(8,128)(2,1)}) %all-gather.15.cloned.1.call-update) | async-done | bytes 4194320 | tf_op jit(solution)/shard_map/all_gather | solution.py:29
  125.9 6.5 copy.73
  152.8 351.5 %while.22 = (s32[]{:T(128)}, bf16[64,4096]{1,0:T(8,128)(2,1)S(1)}, bf16[2,64,4096]{2,1,0:T(8,128)(2,1)}, bf16[128,512]{1,0:T(8,128)(2,1)}, bf16[128,512]{1,0:T(8...) while((s32[]{:T(128)}, bf16[64,4096]{1,0:T(8,128)(2,1)S(1)}, ...), condition=%wide.region_8.9_spmd, body=%wide.region_2.8_spmd.sunk | while | flops 678678656 | bytes 91856312 | solution.py:208
  155.0 14.1 %collective-permute-done = bf16[64,4096]{1,0:T(8,128)(2,1)S(1)} collective-permute-done((bf16[64,4096]{1,0:T(8,128)(2,1)}, bf16[64,4096]{1,0:T(8,128)(2,1)S(1)}, u32[]{:S(2)}, u32[]{:S(2)}) %collective-permute-start) | collective-permute-done | bytes 524320 | tf_op jit(solution)/shard_map/while/body/eval_jaxpr/ppermute | solution.py:43
  171.2 13.8 %collective-permute-done = bf16[64,4096]{1,0:T(8,128)(2,1)S(1)} collective-permute-done((bf16[64,4096]{1,0:T(8,128)(2,1)}, bf16[64,4096]{1,0:T(8,128)(2,1)S(1)}, u32[]{:S(2)}, u32[]{:S(2)}) %collective-permute-start) | collective-permute-done | bytes 524320 | tf_op jit(solution)/shard_map/while/body/eval_jaxpr/ppermute | solution.py:43
  187.2 13.2 %collective-permute-done = bf16[64,4096]{1,0:T(8,128)(2,1)S(1)} collective-permute-done((bf16[64,4096]{1,0:T(8,128)(2,1)}, bf16[64,4096]{1,0:T(8,128)(2,1)S(1)}, u32[]{:S(2)}, u32[]{:S(2)}) %collective-permute-start) | collective-permute-done | bytes 524320 | tf_op jit(solution)/shard_map/while/body/eval_jaxpr/ppermute | solution.py:43
  202.6 12.4 %collective-permute-done = bf16[64,4096]{1,0:T(8,128)(2,1)S(1)} collective-permute-done((bf16[64,4096]{1,0:T(8,128)(2,1)}, bf16[64,4096]{1,0:T(8,128)(2,1)S(1)}, u32[]{:S(2)}, u32[]{:S(2)}) %collective-permute-start) | collective-permute-done | bytes 524320 | tf_op jit(solution)/shard_map/while/body/eval_jaxpr/ppermute | solution.py:43
  217.2 11.5 %collective-permute-done = bf16[64,4096]{1,0:T(8,128)(2,1)S(1)} collective-permute-done((bf16[64,4096]{1,0:T(8,128)(2,1)}, bf16[64,4096]{1,0:T(8,128)(2,1)S(1)}, u32[]{:S(2)}, u32[]{:S(2)}) %collective-permute-start) | collective-permute-done | bytes 524320 | tf_op jit(solution)/shard_map/while/body/eval_jaxpr/ppermute | solution.py:43
  230.9 10.7 %collective-permute-done = bf16[64,4096]{1,0:T(8,128)(2,1)S(1)} collective-permute-done((bf16[64,4096]{1,0:T(8,128)(2,1)}, bf16[64,4096]{1,0:T(8,128)(2,1)S(1)}, u32[]{:S(2)}, u32[]{:S(2)}) %collective-permute-start) | collective-permute-done | bytes 524320 | tf_op jit(solution)/shard_map/while/body/eval_jaxpr/ppermute | solution.py:43
  243.7 186.0 %collective-permute-done = bf16[64,4096]{1,0:T(8,128)(2,1)S(1)} collective-permute-done((bf16[64,4096]{1,0:T(8,128)(2,1)}, bf16[64,4096]{1,0:T(8,128)(2,1)S(1)}, u32[]{:S(2)}, u32[]{:S(2)}) %collective-permute-start) | collective-permute-done | bytes 524320 | tf_op jit(solution)/shard_map/while/body/eval_jaxpr/ppermute | solution.py:43
  429.7 26.1 %conditional.2 = (bf16[64,4096]{1,0:T(8,128)(2,1)}, bf16[2,64,4096]{2,1,0:T(8,128)(2,1)}, bf16[128,512]{1,0:T(8,128)(2,1)}, bf16[128,512]{1,0:T(8,128)(2,1)}, f32[4096]{0:T(1024)}) conditional(s32[]{:T(128)} %convert_element_type.231, (bf16[2,64,4096]{2,1,0:T(8,128)(2,1)}, bf16[128,512]{1,0:T(8,128)(2,1)}, bf16[128,512]{1,0:T(8,128)(2,1)}, ...), branch_computations={%region_3.3_spmd, %region_4.7_spmd} | conditional | flops 678678656 | bytes 89758680 | solution.py:195
  436.6 4.6 fusion.29
  457.1 10.7 %collective-permute-done = bf16[64,4096]{1,0:T(8,128)(2,1)S(1)} collective-permute-done((bf16[64,4096]{1,0:T(8,128)(2,1)}, bf16[64,4096]{1,0:T(8,128)(2,1)S(1)}, u32[]{:S(2)}, u32[]{:S(2)}) %collective-permute-start) | collective-permute-done | bytes 524320 | tf_op jit(solution)/shard_map/while/body/eval_jaxpr/ppermute | solution.py:43
  467.8 26.1 %conditional.2 = (bf16[64,4096]{1,0:T(8,128)(2,1)}, bf16[2,64,4096]{2,1,0:T(8,128)(2,1)}, bf16[128,512]{1,0:T(8,128)(2,1)}, bf16[128,512]{1,0:T(8,128)(2,1)}, f32[4096]{0:T(1024)}) conditional(s32[]{:T(128)} %convert_element_type.231, (bf16[2,64,4096]{2,1,0:T(8,128)(2,1)}, bf16[128,512]{1,0:T(8,128)(2,1)}, bf16[128,512]{1,0:T(8,128)(2,1)}, ...), branch_computations={%region_3.3_spmd, %region_4.7_spmd} | conditional | flops 678678656 | bytes 89758680 | solution.py:195
  474.7 4.6 fusion.29
  495.2 9.2 %collective-permute-done = bf16[64,4096]{1,0:T(8,128)(2,1)S(1)} collective-permute-done((bf16[64,4096]{1,0:T(8,128)(2,1)}, bf16[64,4096]{1,0:T(8,128)(2,1)S(1)}, u32[]{:S(2)}, u32[]{:S(2)}) %collective-permute-start) | collective-permute-done | bytes 524320 | tf_op jit(solution)/shard_map/while/body/eval_jaxpr/ppermute | solution.py:43
  513.9 11.7 %copy.87 = bf16[4096,1025]{1,0:T(8,128)(2,1)} copy(bf16[4096,1025]{0,1:T(8,128)(2,1)} %pad_maximum_fusion) | data formatting | bytes 16793600
  528.5 156.1 %reduce-scatter.4.cloned.1.call-done = bf16[128,1025]{1,0:T(8,128)(2,1)} async-done(((bf16[4096,1025]{1,0:T(8,128)(2,1)}), bf16[128,1025]{1,0:T(8,128)(2,1)}) %reduce-scatter.4.cloned.1.call-update) | async-done | bytes 262416
  (186 shorter events, 122.0 us)
Async XLA Ops:
  7.2 48.6 %copy-start.12 = (bf16[1,2,64,4096]{3,2,1,0:T(8,128)(2,1)S(1)}, bf16[1,2,64,4096]{3,2,1,0:T(8,128)(2,1)}, u32[]{:S(2)}) copy-start(bf16[1,2,64,4096]{3,2,1,0:T(8,128)(2,1)} %param.10) | copy-start | bytes 3145732
  7.2 48.5 %all-gather.13.cloned.1.call-start = ((), (), s32[]{:S(2)}) async-start(), calls=%async_computation.1 | async-start | bytes 2359296 | tf_op jit(solution)/shard_map/all_gather | solution.py:29
  15.8 81.1 %all-gather.17.cloned.1.call-start = ((), (), s32[]{:S(2)}) async-start(), calls=%async_computation.3 | async-start | bytes 2359296 | tf_op jit(solution)/shard_map/all_gather | solution.py:29
  22.5 98.8 %all-gather.15.cloned.1.call-start = ((), (), s32[]{:S(2)}) async-start(), calls=%async_computation.2 | async-start | bytes 6291456 | tf_op jit(solution)/shard_map/all_gather | solution.py:29
  55.7 87.9 %all-gather.19.cloned.1.call-start = ((), (), s32[]{:S(2)}) async-start(), calls=%async_computation.4 | async-start | bytes 6291456 | tf_op jit(solution)/shard_map/all_gather | solution.py:29
  56.0 30.4 %copy-start.5 = (f32[1,2,64,4096]{3,2,1,0:T(8,128)}, f32[1,2,64,4096]{3,2,1,0:T(8,128)S(1)}, u32[]{:S(2)}) copy-start(f32[1,2,64,4096]{3,2,1,0:T(8,128)S(1)} %convert_element_type.149) | copy-start | bytes 6291460
  86.5 10.5 %copy-start.11 = (f32[16,8,32,128]{3,2,1,0:T(8,128)S(1)}, f32[16,8,32,128]{3,2,1,0:T(8,128)}, u32[]{:S(2)}) copy-start(f32[16,8,32,128]{3,2,1,0:T(8,128)} %copy.99) | copy-start | bytes 6291460
  96.9 587.7 %reduce-scatter.4.cloned.1.call-start = ((), (), s32[]{:S(2)}) async-start(), calls=%async_computation.5 | async-start | bytes 9732096
  102.9 29.4 %copy-start.13 = (bf16[1,2,64,4096]{3,2,1,0:T(8,128)(2,1)}, bf16[1,2,64,4096]{3,2,1,0:T(8,128)(2,1)S(1)}, u32[]{:S(2)}) copy-start(bf16[1,2,64,4096]{3,2,1,0:T(8,128)(2,1)S(1)} %multiply_convert_fusion.2) | copy-start | bytes 3145732
  132.4 4.8 copy-start.19
  143.6 4.8 copy-start.14
  153.7 15.4 %collective-permute-start = (bf16[64,4096]{1,0:T(8,128)(2,1)}, bf16[64,4096]{1,0:T(8,128)(2,1)S(1)}, u32[]{:S(2)}, u32[]{:S(2)}) collective-permute-start(bf16[64,4096]{1,0:T(8,128)(2,1)} %get-tuple-element.834), channel_id=1, source_target_pairs={{32,0},{64,32},{96,64},{128,96},{160,128},{192,160},{224,192},{33,... | collective-permute-start | bytes 1572872 | tf_op jit(solution)/shard_map/while/body/eval_jaxpr/ppermute | solution.py:43
  169.9 15.1 %collective-permute-start = (bf16[64,4096]{1,0:T(8,128)(2,1)}, bf16[64,4096]{1,0:T(8,128)(2,1)S(1)}, u32[]{:S(2)}, u32[]{:S(2)}) collective-permute-start(bf16[64,4096]{1,0:T(8,128)(2,1)} %get-tuple-element.834), channel_id=1, source_target_pairs={{32,0},{64,32},{96,64},{128,96},{160,128},{192,160},{224,192},{33,... | collective-permute-start | bytes 1572872 | tf_op jit(solution)/shard_map/while/body/eval_jaxpr/ppermute | solution.py:43
  185.9 14.5 %collective-permute-start = (bf16[64,4096]{1,0:T(8,128)(2,1)}, bf16[64,4096]{1,0:T(8,128)(2,1)S(1)}, u32[]{:S(2)}, u32[]{:S(2)}) collective-permute-start(bf16[64,4096]{1,0:T(8,128)(2,1)} %get-tuple-element.834), channel_id=1, source_target_pairs={{32,0},{64,32},{96,64},{128,96},{160,128},{192,160},{224,192},{33,... | collective-permute-start | bytes 1572872 | tf_op jit(solution)/shard_map/while/body/eval_jaxpr/ppermute | solution.py:43
  201.3 13.7 %collective-permute-start = (bf16[64,4096]{1,0:T(8,128)(2,1)}, bf16[64,4096]{1,0:T(8,128)(2,1)S(1)}, u32[]{:S(2)}, u32[]{:S(2)}) collective-permute-start(bf16[64,4096]{1,0:T(8,128)(2,1)} %get-tuple-element.834), channel_id=1, source_target_pairs={{32,0},{64,32},{96,64},{128,96},{160,128},{192,160},{224,192},{33,... | collective-permute-start | bytes 1572872 | tf_op jit(solution)/shard_map/while/body/eval_jaxpr/ppermute | solution.py:43
  215.9 12.8 %collective-permute-start = (bf16[64,4096]{1,0:T(8,128)(2,1)}, bf16[64,4096]{1,0:T(8,128)(2,1)S(1)}, u32[]{:S(2)}, u32[]{:S(2)}) collective-permute-start(bf16[64,4096]{1,0:T(8,128)(2,1)} %get-tuple-element.834), channel_id=1, source_target_pairs={{32,0},{64,32},{96,64},{128,96},{160,128},{192,160},{224,192},{33,... | collective-permute-start | bytes 1572872 | tf_op jit(solution)/shard_map/while/body/eval_jaxpr/ppermute | solution.py:43
  229.6 12.0 %collective-permute-start = (bf16[64,4096]{1,0:T(8,128)(2,1)}, bf16[64,4096]{1,0:T(8,128)(2,1)S(1)}, u32[]{:S(2)}, u32[]{:S(2)}) collective-permute-start(bf16[64,4096]{1,0:T(8,128)(2,1)} %get-tuple-element.834), channel_id=1, source_target_pairs={{32,0},{64,32},{96,64},{128,96},{160,128},{192,160},{224,192},{33,... | collective-permute-start | bytes 1572872 | tf_op jit(solution)/shard_map/while/body/eval_jaxpr/ppermute | solution.py:43
  242.4 187.3 %collective-permute-start = (bf16[64,4096]{1,0:T(8,128)(2,1)}, bf16[64,4096]{1,0:T(8,128)(2,1)S(1)}, u32[]{:S(2)}, u32[]{:S(2)}) collective-permute-start(bf16[64,4096]{1,0:T(8,128)(2,1)} %get-tuple-element.834), channel_id=1, source_target_pairs={{32,0},{64,32},{96,64},{128,96},{160,128},{192,160},{224,192},{33,... | collective-permute-start | bytes 1572872 | tf_op jit(solution)/shard_map/while/body/eval_jaxpr/ppermute | solution.py:43
  429.7 4.7 copy-start.7
  444.5 3.8 copy-start.4
  444.5 3.8 copy-start.6
  455.8 12.0 %collective-permute-start = (bf16[64,4096]{1,0:T(8,128)(2,1)}, bf16[64,4096]{1,0:T(8,128)(2,1)S(1)}, u32[]{:S(2)}, u32[]{:S(2)}) collective-permute-start(bf16[64,4096]{1,0:T(8,128)(2,1)} %get-tuple-element.834), channel_id=1, source_target_pairs={{32,0},{64,32},{96,64},{128,96},{160,128},{192,160},{224,192},{33,... | collective-permute-start | bytes 1572872 | tf_op jit(solution)/shard_map/while/body/eval_jaxpr/ppermute | solution.py:43
  467.8 4.7 copy-start.7
  493.9 10.5 %collective-permute-start = (bf16[64,4096]{1,0:T(8,128)(2,1)}, bf16[64,4096]{1,0:T(8,128)(2,1)S(1)}, u32[]{:S(2)}, u32[]{:S(2)}) collective-permute-start(bf16[64,4096]{1,0:T(8,128)(2,1)} %get-tuple-element.834), channel_id=1, source_target_pairs={{32,0},{64,32},{96,64},{128,96},{160,128},{192,160},{224,192},{33,... | collective-permute-start | bytes 1572872 | tf_op jit(solution)/shard_map/while/body/eval_jaxpr/ppermute | solution.py:43
  (25 other events, 63.0 us)
Sparse Core Ops, SparseCore 0:
  15.9 39.7 all-gather.12
  57.5 39.3 all-gather.16
  98.7 22.5 all-gather.14
  122.9 20.2 all-gather.18
  525.8 158.7 reduce-scatter.3
where the time goes:
time: 700 us; the launch traced here: 695 us
  waiting for transfers between devices  499 us (71%)
  local copies, waits for them, and re-layouts  56.9 us (8%)
  matrix products  45.5 us (6%)
  blocking collectives  42.6 us (6%)
  other arithmetic  24.6 us (4%)
  between operations  14 us (2%)
  starting transfers between devices  11.7 us (2%)
    ppermute x9, waiting for transfers between devices, from_behind(): lax.ppermute(value, axis, [(source, source + steps) for source in range(f...  282 us
    unnamed x6, waiting for transfers between devices  156 us
    all_gather x4, waiting for transfers between devices, gather_in_order(): parts = lax.all_gather(parts, axes[k])  61.1 us
    all_gather x5, blocking collectives, gather_in_order(): parts = lax.all_gather(parts, axes[k])  42.6 us
    unnamed x32, local copies, waits for them, and re-layouts  19.5 us
    dot_general x4, matrix products, contract_cols(): lax.dot_general(left, right, (((1,), (1,)), ((), ())), preferred_element_...  16 us
  transfers between devices with their start and end apart: 14, of which 13 were waited for; matrix products, arithmetic and copies ran while one was open for 5% of the time, Pallas kernels for 0%

commit v1 on v0

v1 whole, which is shorter than its diff:
```python
import functools
import math

import jax
import jax.numpy as jnp
import numpy as np
from jax import lax
from jax.experimental import pallas as pl
from jax.experimental.pallas import tpu as pltpu
from jax.sharding import Mesh
from jax.sharding import PartitionSpec as P

MESH_ID = pl.DeviceIdType.MESH
KV_HEADS = 4
GROUP = 8
HEAD_DIM = 128
SECTION = ("y", "xl")
DP = ("xh", "z", "c")
eps = 1e-05
rope_base = 500000.0
VMEM_LIMIT = 60 * 1024 * 1024
F32 = jnp.float32
BF16 = jnp.bfloat16


def rope_tables(length, head_dim):
    half = head_dim // 2
    exponent = -(np.arange(half, dtype=np.float32) * np.float32(2.0) / np.float32(head_dim))
    frequency = np.power(np.float32(rope_base), exponent).astype(np.float32)
    angles = np.arange(length, dtype=np.float32)[:, None] * frequency[None, :]
    cosine, sine = np.cos(angles), np.sin(angles)
    return (
        np.concatenate([cosine, cosine], axis=-1).astype(np.float32),
        np.concatenate([-sine, sine], axis=-1).astype(np.float32),
    )


def greet(peers):
    barrier = pltpu.get_barrier_semaphore()
    for peer in peers:
        pl.semaphore_signal(barrier, inc=1, device_id=peer, device_id_type=MESH_ID)
    pl.semaphore_wait(barrier, len(peers))


def remote(src, dst, send, recv, peer):
    return pltpu.make_async_remote_copy(
        src_ref=src, dst_ref=dst, send_sem=send, recv_sem=recv, device_id=peer, device_id_type=MESH_ID
    )


def nn(a, b):
    return lax.dot_general(a, b, (((1,), (0,)), ((), ())), preferred_element_type=F32)


def nt(a, b):
    return lax.dot_general(a, b, (((1,), (1,)), ((), ())), preferred_element_type=F32)


def tn(a, b):
    return lax.dot_general(a, b, (((0,), (0,)), ((), ())), preferred_element_type=F32)


def gather_kernel(nz, *refs):
    sources, fulls = refs[0:3], refs[3:6]
    xs, xr, zs, zr, ds, dr = refs[6:]
    xh, z, c = lax.axis_index("xh"), lax.axis_index("z"), lax.axis_index("c")
    up, down = lax.rem(z + 1, nz), lax.rem(z + nz - 1, nz)
    across, partner = {"xh": 1 - xh}, {"c": 1 - c}
    toward = ({"z": up}, {"z": down})
    long_way, short_way = nz // 2, nz - 1 - nz // 2
    hops = ((long_way, short_way), (short_way, long_way), (long_way, short_way))
    greet([across, partner, toward[0], toward[1]])
    sends = []

    def push(copy):
        copy.start()
        sends.append(copy)

    def place(p, src, steps):
        row = xh if src == 0 else 1 - xh
        return fulls[p].at[row, lax.rem(z + steps + nz, nz), c]

    def share(p, src, data, slot, index):
        push(remote(data, slot, ds.at[p, src, index], dr.at[p, src, index], partner))

    for p in range(3):
        slot = place(p, 0, 0)
        push(remote(sources[p], slot, xs.at[p], xr.at[p], across))
        for d in range(2):
            push(remote(sources[p], slot, zs.at[d, 0, 0, p], zr.at[d, 0, 0, p], toward[d]))
    for p in range(3):
        share(p, 0, sources[p], place(p, 0, 0), 0)
    for p in range(3):
        fulls[p][xh, z, c] = sources[p][...]
    for p in range(3):
        slot = place(p, 1, 0)
        remote(slot, slot, xs.at[p], xr.at[p], across).wait_recv()
        for d in range(2):
            push(remote(slot, slot, zs.at[d, 0, 1, p], zr.at[d, 0, 1, p], toward[d]))
        share(p, 1, slot, slot, 0)
    for t in range(1, long_way + 1):
        for src in range(2):
            for p in range(3):
                for d in range(2):
                    if t > hops[p][d]:
                        continue
                    slot = place(p, src, -t if d == 0 else t)
                    remote(
                        slot, slot, zs.at[d, t - 1, src, p], zr.at[d, t - 1, src, p], toward[d]
                    ).wait_recv()
                    if t < hops[p][d]:
                        push(remote(slot, slot, zs.at[d, t, src, p], zr.at[d, t, src, p], toward[d]))
                    share(p, src, slot, slot, 1 + 4 * d + t - 1)
    for p in range(3):
        for src in range(2):
            row = xh if src == 0 else 1 - xh
            for d in range(2):
                for t in range(hops[p][d] + 1):
                    if t == 0 and d == 1:
                        continue
                    index = 0 if t == 0 else 1 + 4 * d + t - 1
                    steps = -t if d == 0 else t
                    slot = fulls[p].at[row, lax.rem(z + steps + nz, nz), 1 - c]
                    remote(slot, slot, ds.at[p, src, index], dr.at[p, src, index], partner).wait_recv()
    for copy in sends:
        copy.wait_send()


def gather_weights(key_weight, value_weight, gain, nxh, nz, nc):
    sources = (key_weight, value_weight, gain)
    return pl.pallas_call(
        functools.partial(gather_kernel, nz),
        out_shape=[jax.ShapeDtypeStruct((nxh, nz, nc, *a.shape), a.dtype) for a in sources],
        in_specs=[pl.BlockSpec(memory_space=pltpu.VMEM)] * 3,
        out_specs=[pl.BlockSpec(memory_space=pltpu.VMEM)] * 3,
        scratch_shapes=[
            pltpu.SemaphoreType.DMA((3,)),
            pltpu.SemaphoreType.DMA((3,)),
            pltpu.SemaphoreType.DMA((2, 4, 2, 3)),
            pltpu.SemaphoreType.DMA((2, 4, 2, 3)),
            pltpu.SemaphoreType.DMA((3, 2, 9)),
            pltpu.SemaphoreType.DMA((3, 2, 9)),
        ],
        compiler_params=pltpu.CompilerParams(
            collective_id=0, has_side_effects=True, vmem_limit_bytes=VMEM_LIMIT
        ),
        name="gather_weights",
    )(*sources)


def relay_kernel(
    ny, nz, x_ref, cot_ref, wk_ref, wv_ref, gain_ref, cos_ref, sin_ref,
    low_ref, rows_ref, kv_ref, colsum_ref,
    up_ref, normed_s, out_rows, key_s, value_s, query_s, prob_s, inv_s, qb_s, gsum_s,
    us, ur, ns, nr,
):
    y, xl = lax.axis_index("y"), lax.axis_index("xl")
    xh, c = lax.axis_index("xh"), lax.axis_index("c")
    section, sections = y * 2 + xl, ny * 2
    batches, tokens, width = x_ref.shape
    kv_width = wk_ref.shape[1]
    block = GROUP * HEAD_DIM
    scale = 1.0 / math.sqrt(HEAD_DIM)
    below = lax.rem(section + sections - 1, sections)
    above = lax.rem(section + 1, sections)
    lower_peer = {"y": below // 2, "xl": lax.rem(below, 2)}
    upper_peer = {"y": above // 2, "xl": lax.rem(above, 2)}
    near = ((xh, 1 - c), (1 - xh, c), (1 - xh, 1 - c))
    row_peers = [{"xh": a, "c": b} for a, b in near]
    greet([lower_peer, upper_peer] + row_peers)
    cosine, sine = cos_ref[...], sin_ref[...]

    def rotate(v):
        return v * cosine + pltpu.roll(v, HEAD_DIM // 2, axis=1) * sine

    def unrotate(v):
        return v * cosine - pltpu.roll(v, HEAD_DIM // 2, axis=1) * sine

    def head(h):
        return slice(h * HEAD_DIM, (h + 1) * HEAD_DIM)

    gsum_s[...] = jnp.zeros_like(gsum_s)
    for i in range(batches):
        here = slice(i * tokens, (i + 1) * tokens)
        total = jnp.zeros((tokens, HEAD_DIM), F32)
        for h in range(width // HEAD_DIM):
            piece = x_ref[i, :, head(h)].astype(F32)
            total = total + piece * piece
        inv = lax.rsqrt(jnp.sum(total, axis=-1, keepdims=True) * (1.0 / width) + eps)
        inv_s[here, :] = jnp.broadcast_to(inv, (tokens, HEAD_DIM))
        for h in range(width // HEAD_DIM):
            piece = x_ref[i, :, head(h)].astype(F32)
            normed = (piece * inv * gain_ref[:, head(h)]).astype(BF16)
            normed_s[here, head(h)] = normed
            a, zz, b = h // (2 * nz), (h // 2) % nz, h % 2
            out_rows[a, b, here, head(zz)] = normed
            rot = rotate(normed.astype(F32)).astype(BF16)
            query_s[i, h // GROUP, slice((h % GROUP) * tokens, (h % GROUP + 1) * tokens), :] = rot
    rows_ref[xh, c] = out_rows[xh, c]
    row_sends = []
    for n, (a, b) in enumerate(near):
        copy = remote(out_rows.at[a, b], rows_ref.at[xh, c], ns.at[n], nr.at[n], row_peers[n])
        copy.start()
        row_sends.append(copy)
    key_pre = nn(normed_s[...], wk_ref[...])
    value_pre = nn(normed_s[...], wv_ref[...])
    for i in range(batches):
        here = slice(i * tokens, (i + 1) * tokens)
        for k in range(KV_HEADS):
            key_s[i, k] = rotate(key_pre[here, head(k)]).astype(BF16)
            value_s[i, k] = value_pre[here, head(k)].astype(BF16)
    m_at = lax.broadcasted_iota(jnp.int32, (tokens, GROUP * tokens), 0)
    l_at = lax.rem(lax.broadcasted_iota(jnp.int32, (tokens, GROUP * tokens), 1), tokens)
    causal = m_at <= l_at
    for i in range(batches):
        for k in range(KV_HEADS):
            scores = nt(key_s[i, k], query_s[i, k]) * scale
            raised = jnp.where(causal, jnp.exp(scores), 0.0)
            prob_s[i, k] = raised / jnp.sum(raised, axis=0, keepdims=True)

    @pl.when(section == sections - 1)
    def _():
        up_ref[...] = cot_ref[...]

    def chunk(ref, i, k):
        return ref.at[i, :, pl.ds(k * block, block)]

    def outgoing(i, k):
        return remote(chunk(low_ref, i, k), chunk(up_ref, i, k), us.at[i, k], ur.at[i, k], lower_peer)

    def one_batch(i, carry):
        start = pl.multiple_of(i * tokens, tokens)
        here = pl.ds(start, tokens)
        for k in range(KV_HEADS):

            @pl.when(section < sections - 1)
            def _():
                remote(
                    chunk(low_ref, i, k), chunk(up_ref, i, k), us.at[i, k], ur.at[i, k], lower_peer
                ).wait_recv()

            upper = jnp.concatenate(
                [up_ref[i, :, head(k * GROUP + h)] for h in range(GROUP)], axis=0
            )
            prob = prob_s[i, k]
            grad_prob = nt(value_s[i, k], upper)
            grad_value = nn(prob.astype(BF16), upper).astype(BF16)
            row_dot = jnp.sum(prob * grad_prob, axis=0, keepdims=True)
            grad_score = (prob * (grad_prob - row_dot) * scale).astype(BF16)
            grad_query = tn(grad_score, key_s[i, k])
            grad_key = nn(grad_score, query_s[i, k])
            kv_ref[here, head(k)] = unrotate(grad_key).astype(BF16)
            kv_ref[here, slice(kv_width + k * HEAD_DIM, kv_width + (k + 1) * HEAD_DIM)] = grad_value
            for h in range(GROUP):
                qb_s[:, head(k * GROUP + h)] = unrotate(
                    grad_query[h * tokens : (h + 1) * tokens, :]
                )
        key_back = kv_ref[here, 0:kv_width]
        value_flat = kv_ref[here, kv_width : 2 * kv_width]
        inv = inv_s[here, :][:, 0:1]
        mean = jnp.zeros((tokens, HEAD_DIM), F32)
        for k in range(KV_HEADS):
            cols = slice(k * block, (k + 1) * block)
            projected = nt(key_back, wk_ref[cols, :]) + nt(value_flat, wv_ref[cols, :])
            for h in range(GROUP):
                at = head(k * GROUP + h)
                grad_normed = qb_s[:, at] + projected[:, head(h)]
                qb_s[:, at] = grad_normed
                term = grad_normed * x_ref[i, :, at].astype(F32) * inv
                gsum_s[:, at] += jnp.sum(term.reshape(tokens // 8, 8, HEAD_DIM), axis=0)
                mean = mean + term * gain_ref[:, at]
        row_mean = jnp.sum(mean, axis=-1, keepdims=True) * (1.0 / width)
        drop = inv * inv * row_mean
        for k in range(KV_HEADS):
            for h in range(GROUP):
                at = head(k * GROUP + h)
                low_ref[i, :, at] = (
                    up_ref[i, :, at].astype(F32)
                    + inv * gain_ref[:, at] * qb_s[:, at]
                    - x_ref[i, :, at].astype(F32) * drop
                ).astype(BF16)

            @pl.when(section > 0)
            def _():
                outgoing(i, k).start()

        return carry

    lax.fori_loop(0, batches, one_batch, 0)
    column = jnp.sum(gsum_s[...], axis=0, keepdims=True)
    pieces = []
    for a in range(2):
        for b in range(2):
            pieces.append(
                jnp.concatenate(
                    [column[:, head(a * 2 * nz + 2 * zz + b)] for zz in range(nz)], axis=1
                )
            )
    pieces.append(jnp.zeros((12, nz * HEAD_DIM), F32))
    colsum_ref[...] = jnp.concatenate(pieces, axis=0).astype(BF16)
    for n, (a, b) in enumerate(near):
        remote(out_rows.at[a, b], rows_ref.at[a, b], ns.at[n], nr.at[n], row_peers[n]).wait_recv()
    for copy in row_sends:
        copy.wait_send()

    @pl.when(section > 0)
    def _():
        for i in range(batches):
            for k in range(KV_HEADS):
                outgoing(i, k).wait_send()


def relay(x, cot, wk, wv, gain, ny, nz):
    batches, tokens, width = x.shape
    kv_width = wk.shape[1]
    cosine, sine = rope_tables(tokens, HEAD_DIM)
    rows = batches * tokens
    return pl.pallas_call(
        functools.partial(relay_kernel, ny, nz),
        out_shape=[
            jax.ShapeDtypeStruct((batches, tokens, width), BF16),
            jax.ShapeDtypeStruct((2, 2, rows, nz * HEAD_DIM), BF16),
            jax.ShapeDtypeStruct((rows, 2 * kv_width), BF16),
            jax.ShapeDtypeStruct((16, nz * HEAD_DIM), BF16),
        ],
        in_specs=[pl.BlockSpec(memory_space=pltpu.VMEM)] * 7,
        out_specs=[pl.BlockSpec(memory_space=pltpu.VMEM)] * 4,
        scratch_shapes=[
            pltpu.VMEM((batches, tokens, width), BF16),
            pltpu.VMEM((rows, width), BF16),
            pltpu.VMEM((2, 2, rows, nz * HEAD_DIM), BF16),
            pltpu.VMEM((batches, KV_HEADS, tokens, HEAD_DIM), BF16),
            pltpu.VMEM((batches, KV_HEADS, tokens, HEAD_DIM), BF16),
            pltpu.VMEM((batches, KV_HEADS, GROUP * tokens, HEAD_DIM), BF16),
            pltpu.VMEM((batches, KV_HEADS, tokens, GROUP * tokens), F32),
            pltpu.VMEM((rows, HEAD_DIM), F32),
            pltpu.VMEM((tokens, width), F32),
            pltpu.VMEM((8, width), F32),
            pltpu.SemaphoreType.DMA((batches, KV_HEADS)),
            pltpu.SemaphoreType.DMA((batches, KV_HEADS)),
            pltpu.SemaphoreType.DMA((3,)),
            pltpu.SemaphoreType.DMA((3,)),
        ],
        compiler_params=pltpu.CompilerParams(
            collective_id=1, has_side_effects=True, vmem_limit_bytes=VMEM_LIMIT
        ),
        name="relay",
    )(x, cot, wk, wv, gain, jnp.asarray(cosine), jnp.asarray(sine))


SUBS = 2


def reduce_kernel(
    nz, rows_ref, kv_ref, colsum_ref, key_out, value_out, gain_out,
    kv_all, col_all, sbuf, rbuf, gsend, grecv, ks, kr, cs, cr, zs, zr, gs, gr,
):
    xh, z, c = lax.axis_index("xh"), lax.axis_index("z"), lax.axis_index("c")
    across, partner = {"xh": 1 - xh}, {"c": 1 - c}
    toward = ({"z": lax.rem(z + 1, nz)}, {"z": lax.rem(z + nz - 1, nz)})
    ring = [{"z": lax.rem(z + s, nz)} for s in range(1, nz)]
    greet([across, partner] + ring)
    kv_width = key_out.shape[1]
    depth = key_out.shape[0]
    part = depth // SUBS
    sends = []

    def push(copy):
        copy.start()
        sends.append(copy)

    for n, peer in enumerate((partner, across)):
        push(remote(kv_ref, kv_all.at[xh, c], ks.at[n], kr.at[n], peer))
        push(remote(colsum_ref, col_all.at[xh, c], cs.at[n], cr.at[n], peer))
    kv_all[xh, c] = kv_ref[...]
    col_all[xh, c] = colsum_ref[...]
    slot, cslot = kv_all.at[1 - xh, c], col_all.at[1 - xh, c]
    remote(slot, slot, ks.at[1], kr.at[1], across).wait_recv()
    push(remote(slot, slot, ks.at[2], kr.at[2], partner))
    remote(cslot, cslot, cs.at[1], cr.at[1], across).wait_recv()
    push(remote(cslot, cslot, cs.at[2], cr.at[2], partner))
    for n, a in ((0, xh), (2, 1 - xh)):
        slot, cslot = kv_all.at[a, 1 - c], col_all.at[a, 1 - c]
        remote(slot, slot, ks.at[n], kr.at[n], partner).wait_recv()
        remote(cslot, cslot, cs.at[n], cr.at[n], partner).wait_recv()

    def partial(target, p):
        at = pl.ds(pl.multiple_of(target * HEAD_DIM, HEAD_DIM), HEAD_DIM)
        total = None
        for a in range(2):
            for b in range(2):
                one = tn(rows_ref[a, b, :, at], kv_all[a, b, :, p * kv_width : (p + 1) * kv_width])
                total = one if total is None else total + one
        return total

    long_way, short_way = nz // 2, nz - 1 - nz // 2
    hops = ((long_way, short_way), (short_way, long_way))

    def ring_copy(d, p, t, s):
        return remote(
            sbuf.at[d, p, t, s], rbuf.at[d, p, t, s], zs.at[d, p, t, s], zr.at[d, p, t, s], toward[d]
        )

    for t in range(long_way):
        for p in range(2):
            for d in range(2):
                if t >= hops[p][d]:
                    continue
                steps = hops[p][d] - t
                target = lax.rem(z + (steps if d == 0 else nz - steps), nz)
                mine = partial(target, p)
                for s in range(SUBS):
                    piece = mine[s * part : (s + 1) * part, :]
                    if t > 0:
                        ring_copy(d, p, t - 1, s).wait_recv()
                        piece = piece + rbuf[d, p, t - 1, s].astype(F32)
                    sbuf[d, p, t, s] = piece.astype(BF16)
                    push(ring_copy(d, p, t, s))
        if t == 0:
            own = lax.broadcasted_iota(jnp.int32, (16, nz * HEAD_DIM), 0) == xh * 2 + c
            totals = jnp.zeros((16, nz * HEAD_DIM), F32)
            for a in range(2):
                for b in range(2):
                    totals = totals + col_all[a, b].astype(F32)
            line = jnp.sum(jnp.where(own, totals, 0.0), axis=0, keepdims=True)
            for zz in range(nz):
                gsend[zz] = jnp.broadcast_to(
                    line[:, zz * HEAD_DIM : (zz + 1) * HEAD_DIM], (8, HEAD_DIM)
                )
            for s in range(1, nz):
                push(
                    remote(
                        gsend.at[lax.rem(z + s, nz)], grecv.at[s - 1], gs.at[s - 1], gr.at[s - 1],
                        ring[s - 1],
                    )
                )
    outs = (key_out, value_out)
    for p in range(2):
        mine = partial(z, p)
        for s in range(SUBS):
            piece = mine[s * part : (s + 1) * part, :]
            for d in range(2):
                last = hops[p][d] - 1
                ring_copy(d, p, last, s).wait_recv()
                piece = piece + rbuf[d, p, last, s].astype(F32)
            outs[p][s * part : (s + 1) * part, :] = piece
    column = gsend[z]
    for s in range(1, nz):
        remote(
            gsend.at[0], grecv.at[s - 1], gs.at[s - 1], gr.at[s - 1], ring[s - 1]
        ).wait_recv()
        column = column + grecv[s - 1]
    gain_out[...] = column
    for copy in sends:
        copy.wait_send()


def reduce_weights(rows, kv, colsum, nz):
    total_rows, both = kv.shape
    half = both // 2
    ring = (2, 2, nz // 2, SUBS)
    return pl.pallas_call(
        functools.partial(reduce_kernel, nz),
        out_shape=[
            jax.ShapeDtypeStruct((HEAD_DIM, half), F32),
            jax.ShapeDtypeStruct((HEAD_DIM, half), F32),
            jax.ShapeDtypeStruct((8, HEAD_DIM), F32),
        ],
        in_specs=[pl.BlockSpec(memory_space=pltpu.VMEM)] * 3,
        out_specs=[pl.BlockSpec(memory_space=pltpu.VMEM)] * 3,
        scratch_shapes=[
            pltpu.VMEM((2, 2, total_rows, both), BF16),
            pltpu.VMEM((2, 2, 16, colsum.shape[1]), BF16),
            pltpu.VMEM((*ring, HEAD_DIM // SUBS, half), BF16),
            pltpu.VMEM((*ring, HEAD_DIM // SUBS, half), BF16),
            pltpu.VMEM((nz, 8, HEAD_DIM), F32),
            pltpu.VMEM((nz - 1, 8, HEAD_DIM), F32),
            pltpu.SemaphoreType.DMA((3,)),
            pltpu.SemaphoreType.DMA((3,)),
            pltpu.SemaphoreType.DMA((3,)),
            pltpu.SemaphoreType.DMA((3,)),
            pltpu.SemaphoreType.DMA(ring),
            pltpu.SemaphoreType.DMA(ring),
            pltpu.SemaphoreType.DMA((nz - 1,)),
            pltpu.SemaphoreType.DMA((nz - 1,)),
        ],
        compiler_params=pltpu.CompilerParams(
            collective_id=2, has_side_effects=True, vmem_limit_bytes=VMEM_LIMIT
        ),
        name="reduce_weights",
    )(rows, kv, colsum)


def solution(mesh):
    sections, dp = mesh.shape["section"], mesh.shape["dp"]
    ny, nz = sections // 2, dp // 4
    split = Mesh(mesh.devices.reshape(ny, 2, 2, nz, 2), ("y", "xl", "xh", "z", "c"))

    def body(inputs, cotangent, norm_gain, key_weight, value_weight, plan):
        _, batches, tokens, width = inputs.shape
        kv_width = key_weight.shape[2]
        own_gain = jnp.broadcast_to(norm_gain[0].astype(F32)[None, :], (8, HEAD_DIM))
        wk, wv, gains = gather_weights(key_weight[0], value_weight[0], own_gain, 2, nz, 2)
        wk, wv = wk.reshape(width, kv_width), wv.reshape(width, kv_width)
        gain = gains[:, :, :, 0, :].reshape(1, width)
        low, rows, kv, colsum = relay(inputs[0], cotangent, wk, wv, gain, ny, nz)
        key_grad, value_grad, gain_grad = reduce_weights(rows, kv, colsum, nz)
        selector = plan[0][:, None] == jnp.arange(batches, dtype=jnp.int32)[None, :]
        ordered = jnp.sum(
            jnp.where(selector[:, :, None, None], low[None], jnp.zeros((), BF16)), axis=1
        )
        return ordered[None], key_grad[None], value_grad[None], gain_grad[0:1]

    placed = (
        P(SECTION, None, DP, None),
        P(None, DP, None),
        P(SECTION, DP),
        P(SECTION, DP, None),
        P(SECTION, DP, None),
        P(SECTION, None),
    )
    return jax.shard_map(
        body,
        mesh=split,
        in_specs=placed,
        out_specs=(
            P(SECTION, None, DP, None),
            P(SECTION, DP, None),
            P(SECTION, DP, None),
            P(SECTION, DP),
        ),
        check_vma=False,
    )
```

time: 700 us -> 239 us (0.34)
  waiting for transfers between devices: 499 us -> 0 us
  Pallas kernels: 0 us -> 229 us
  local copies, waits for them, and re-layouts: 56.9 us -> 4.78 us
  matrix products: 45.5 us -> 0 us
  blocking collectives: 42.6 us -> 0 us
  other arithmetic: 24.6 us -> 3.75 us
  between operations: 14 us -> 0.68 us
  starting transfers between devices: 11.7 us -> 0 us
    ppermute x9 -> x0, waiting for transfers between devices: 282 us -> none  [from_behind(): lax.ppermute(value, axis, [(source, source + steps) for source in range(f...]
    pallas_call x0 -> x3, Pallas kernels: none -> 229 us  [the longest x1 130 us: relay(): pl.pallas_call(functools.partial(relay_kernel, ny, nz), out_shape=[jax.Sh...]
    unnamed x6 -> x0, waiting for transfers between devices: 156 us -> none
    all_gather x4 -> x0, waiting for transfers between devices: 61.1 us -> none  [gather_in_order(): parts = lax.all_gather(parts, axes[k])]
    all_gather x5 -> x0, blocking collectives: 42.6 us -> none  [gather_in_order(): parts = lax.all_gather(parts, axes[k])]
    dot_general x16 -> x0, matrix products: 42.3 us -> none  [the longest x4 16 us: contract_cols(): lax.dot_general(left, right, (((1,), (1,)), ((), ())), preferred_element_...]
    unnamed x32 -> x8, local copies, waits for them, and re-layouts: 19.5 us -> 1.42 us
    ppermute x9 -> x0, starting transfers between devices: 11.5 us -> none  [from_behind(): lax.ppermute(value, axis, [(source, source + steps) for source in range(f...]
  transfers between devices with their start and end apart: 14 -> 0, of which waited for: 13 -> 0; matrix products, arithmetic and copies ran while one was open for 5% -> 0% of each run, Pallas kernels for 0% -> 0%
where the time goes in v1:
time: 239 us
  Pallas kernels  229 us (96%)
  local copies, waits for them, and re-layouts  4.78 us (2%)
  other arithmetic  3.75 us (2%)
    pallas_call x1, Pallas kernels, relay(): pl.pallas_call(functools.partial(relay_kernel, ny, nz), out_shape=[jax.Sh...  130 us
    pallas_call x1, Pallas kernels, gather_weights(): pl.pallas_call(functools.partial(gather_kernel, nz), out_shape=[jax.Shape...  58.1 us
    pallas_call x1, Pallas kernels, reduce_weights(): pl.pallas_call(functools.partial(reduce_kernel, nz), out_shape=[jax.Shape...  41.3 us

profile of v1, /device:TPU:1, one launch (start us, length us, event | category | flops | bytes accessed | tf_op | source)
XLA Modules:
  0.0 238.6 jit_solution(8237014887830040172)
XLA Ops:
  0.6 0.7 bitcast_convert_fusion
  1.3 0.6 broadcast_in_dim.46.refs_2_
  1.9 58.1 %gather_weights.1 = (bf16[2,8,2,128,512]{4,3,2,1,0:T(8,128)(2,1)}, bf16[2,8,2,128,512]{4,3,2,1,0:T(8,128)(2,1)}, f32[2,8,2,8,128]{4,3,2,1,0:T(8,128)}) custom-call(bf16[128,512]{1,0:T(8,128)(2,1)} %bitcast.19, bf16[128,512]{1,0:T(8,128)(2,1)} %bitcast.20, f32[8,128]{1,0:T(8,128)} %broadcast_in_dim.46.refs_2_), custom_call_target="tpu_custom_call" | custom-call | tf_op jit(solution)/shard_map/gather_weights/pallas_call | solution.py:131
  59.9 1.5 slice.6
  61.5 0.0 copy-start.2
  61.5 130.1 %relay.1 = (bf16[2,64,4096]{2,1,0:T(8,128)(2,1)}, bf16[2,2,128,1024]{3,2,1,0:T(8,128)(2,1)}, bf16[128,1024]{1,0:T(8,128)(2,1)}, bf16[16,1024]{1,0:T(8,128)(2,1)}) custom-call(bf16[2,64,4096]{2,1,0:T(8,128)(2,1)} %bitcast.15, bf16[2,64,4096]{2,1,0:T(8,128)(2,1)} %cot_ref.1, bf16[4096,512]{1,0:T(8,128)(2,1)} %bitcast.13, bf16[4096,512]{1,0:T(8,128)(2,1)} %bitcast.14, ...), custom_call_target="tpu_custom_call" | custom-call | tf_op jit(solution)/shard_map/relay/pallas_call | solution.py:318
  191.5 41.3 %reduce_weights.1 = (f32[128,512]{1,0:T(8,128)}, f32[128,512]{1,0:T(8,128)}, f32[8,128]{1,0:T(8,128)}) custom-call(bf16[2,2,128,1024]{3,2,1,0:T(8,128)(2,1)} %get-tuple-element.18.rows_ref, bf16[128,1024]{1,0:T(8,128)(2,1)} %get-tuple-element.19.kv_ref, bf16[16,1024]{1,0:T(8,128)(2,1)} %get-tuple-element.20.colsum_ref), custom_call_target="tpu_custom_call" | custom-call | tf_op jit(solution)/shard_map/reduce_weights/pallas_call | solution.py:462
  232.8 0.0 copy-start.1
  232.9 0.0 copy-start
  232.9 1.3 slice.7
  234.1 0.0 copy-done.2
  234.1 0.1 iota_compare_fusion
  234.2 3.0 %select_reduce_fusion = bf16[2,64,4096]{2,1,0:T(8,128)(2,1)} fusion(pred[2,2]{1,0:T(4,128)(4,1)S(1)} %iota_compare_fusion, bf16[2,64,4096]{2,1,0:T(8,128)(2,1)} %get-tuple-element.17), kind=kLoop, calls=%fused_computation | loop fusion | flops 1572864 | bytes 2097156 | tf_op jit(solution)/shard_map/reduce_sum | solution.py:509
  237.2 0.0 copy-done.1
  237.2 0.7 copy.14
  237.9 0.0 copy-done
  237.9 0.7 copy.15
Async XLA Ops:
  61.5 172.7 %copy-start.2 = (s32[1,2]{1,0:T(1,128)S(1)}, s32[1,2]{1,0:T(1,128)}, u32[]{:S(2)}) copy-start(s32[1,2]{1,0:T(1,128)} %param.13) | copy-start | bytes 28
  232.8 4.4 %copy-start.1 = (f32[128,512]{1,0:T(8,128)S(1)}, f32[128,512]{1,0:T(8,128)}, u32[]{:S(2)}) copy-start(f32[128,512]{1,0:T(8,128)} %get-tuple-element.21) | copy-start | bytes 786436
  232.9 5.1 %copy-start = (f32[128,512]{1,0:T(8,128)S(1)}, f32[128,512]{1,0:T(8,128)}, u32[]{:S(2)}) copy-start(f32[128,512]{1,0:T(8,128)} %get-tuple-element.22) | copy-start | bytes 786436

commit v2 on v1

v2 whole, which is shorter than its diff:
```python
import functools
import math

import jax
import jax.numpy as jnp
import numpy as np
from jax import lax
from jax.experimental import pallas as pl
from jax.experimental.pallas import tpu as pltpu
from jax.sharding import Mesh
from jax.sharding import PartitionSpec as P

MESH_ID = pl.DeviceIdType.MESH
KV_HEADS = 4
GROUP = 8
HEAD_DIM = 128
SECTION = ("y", "xl")
DP = ("xh", "z", "c")
eps = 1e-05
rope_base = 500000.0
VMEM_LIMIT = 60 * 1024 * 1024
F32 = jnp.float32
BF16 = jnp.bfloat16

PIECES = 8
DETOUR = (0, 1, 2)
SEND_ORDER = (0, 4, 1, 5, 2, 6, 7, 3)
KEY_ORDER = (2, 3, 0, 1)
SUBS = 2


def rope_tables(length, head_dim):
    half = head_dim // 2
    exponent = -(np.arange(half, dtype=np.float32) * np.float32(2.0) / np.float32(head_dim))
    frequency = np.power(np.float32(rope_base), exponent).astype(np.float32)
    angles = np.arange(length, dtype=np.float32)[:, None] * frequency[None, :]
    cosine, sine = np.cos(angles), np.sin(angles)
    return (
        np.concatenate([cosine, cosine], axis=-1).astype(np.float32),
        np.concatenate([-sine, sine], axis=-1).astype(np.float32),
    )


def remote(src, dst, send, recv, peer):
    return pltpu.make_async_remote_copy(
        src_ref=src, dst_ref=dst, send_sem=send, recv_sem=recv, device_id=peer, device_id_type=MESH_ID
    )


def nn(a, b):
    return lax.dot_general(a, b, (((1,), (0,)), ((), ())), preferred_element_type=F32)


def nt(a, b):
    return lax.dot_general(a, b, (((1,), (1,)), ((), ())), preferred_element_type=F32)


def tn(a, b):
    return lax.dot_general(a, b, (((0,), (0,)), ((), ())), preferred_element_type=F32)


def head(h):
    return slice(h * HEAD_DIM, (h + 1) * HEAD_DIM)


def kernel(
    ny, nz,
    x_ref, cot_ref, wk_ref, wv_ref, gain_ref, plan_ref, cos_ref, sin_ref,
    low_out, key_out, value_out, gain_out,
    fk, fv, fg, up_ref, low_s, via_ref, normed_s, out_rows, rows_all, key_s, value_s, query_s,
    prob_s, inv_s, qb_s, pre_k, pre_v, kv_s, kv_all, col_s, col_all, sbuf, rbuf, gsend, grecv,
    xs, xr, zs, zr, ws, wr, ds, dr,
    us, ur, vs, vr, fs, ns, nr, ks, kr, cs, cr, rs, rr, gs, gr,
):
    y, xl = lax.axis_index("y"), lax.axis_index("xl")
    xh, z, c = lax.axis_index("xh"), lax.axis_index("z"), lax.axis_index("c")
    section, sections = y * 2 + xl, ny * 2
    batches, tokens, width = x_ref.shape
    kv_width = wk_ref.shape[1]
    heads = width // HEAD_DIM
    scale = 1.0 / math.sqrt(HEAD_DIM)

    def section_peer(steps):
        there = lax.rem(section + sections + steps, sections)
        return {"y": there // 2, "xl": lax.rem(there, 2)}

    below, above = section_peer(-1), section_peer(1)
    two_below, two_above = section_peer(-2), section_peer(2)
    across, partner, corner = {"xh": 1 - xh}, {"c": 1 - c}, {"xh": 1 - xh, "c": 1 - c}
    ring = [{"z": lax.rem(z + s, nz)} for s in range(1, nz)]
    toward = (ring[0], ring[nz - 2])
    long_way, short_way = nz // 2, nz - 1 - nz // 2

    barrier = pltpu.get_barrier_semaphore()
    greeted = [across, partner, corner, below, above, two_below, two_above] + ring
    for peer in greeted:
        pl.semaphore_signal(barrier, inc=1, device_id=peer, device_id_type=MESH_ID)
    pl.semaphore_wait(barrier, len(greeted))

    sends = []

    def push(copy):
        copy.start()
        sends.append(copy)

    cosine, sine = cos_ref[...], sin_ref[...]

    def rotate(v):
        return v * cosine + pltpu.roll(v, HEAD_DIM // 2, axis=1) * sine

    def unrotate(v):
        return v * cosine - pltpu.roll(v, HEAD_DIM // 2, axis=1) * sine

    def gain(h):
        return fg[h // (2 * nz), (h // 2) % nz, h % 2, 0:1, :]

    sources, fulls = (wk_ref, wv_ref, gain_ref), (fk, fv, fg)
    hops = ((long_way, short_way), (short_way, long_way), (long_way, short_way))

    def place(p, src, steps, core=c):
        row = xh if src == 0 else 1 - xh
        return fulls[p].at[row, lax.rem(z + steps + nz, nz), core]

    def index_of(d, t):
        return 0 if t == 0 else 1 + long_way * d + t - 1

    def steps_of(d, t):
        return -t if d == 0 else t

    def share(p, src, data, slot, index):
        push(remote(data, slot, ds.at[p, src, index], dr.at[p, src, index], partner))

    def ring_copy(data, slot, d, t, src, p):
        return remote(data, slot, zs.at[d, t, src, p], zr.at[d, t, src, p], toward[d])

    def first_moves(p):
        slot = place(p, 0, 0)
        if p != 1:
            push(remote(sources[p], slot, xs.at[p], xr.at[p], across))
        else:
            push(remote(sources[p], slot, ws.at[0], wr.at[0], across))
        for d in range(2):
            push(ring_copy(sources[p], slot, d, 0, 0, p))
        share(p, 0, sources[p], slot, 0)
        fulls[p][xh, z, c] = sources[p][...]

    def row_arrival(p):
        slot = place(p, 1, 0)
        remote(slot, slot, xs.at[p], xr.at[p], across).wait_recv()
        for d in range(2):
            push(ring_copy(slot, slot, d, 0, 1, p))
        share(p, 1, slot, slot, 0)

    def ring_arrival(p, src, d, t):
        if t > hops[p][d]:
            return
        slot = place(p, src, steps_of(d, t))
        ring_copy(slot, slot, d, t - 1, src, p).wait_recv()
        if t < hops[p][d]:
            push(ring_copy(slot, slot, d, t, src, p))
        index = index_of(d, t)
        if p == 1:
            push(remote(slot, slot, ws.at[index], wr.at[index], across))
        share(p, src, slot, slot, index)

    def cross_arrival(d, t):
        if t > hops[1][d]:
            return
        index = index_of(d, t)
        slot = place(1, 1, steps_of(d, t))
        remote(slot, slot, ws.at[index], wr.at[index], across).wait_recv()
        share(1, 1, slot, slot, index)

    def shared_arrivals(p):
        for src in range(2):
            for d in range(2):
                for t in range(hops[p][d] + 1):
                    if t == 0 and d == 1:
                        continue
                    index = index_of(d, t)
                    slot = place(p, src, steps_of(d, t), 1 - c)
                    remote(slot, slot, ds.at[p, src, index], dr.at[p, src, index], partner).wait_recv()

    def mean_square(i):
        here = slice(i * tokens, (i + 1) * tokens)
        total = jnp.zeros((tokens, HEAD_DIM), F32)
        for h in range(heads):
            piece = x_ref[i, :, head(h)].astype(F32)
            total = total + piece * piece
        inv = lax.rsqrt(jnp.sum(total, axis=-1, keepdims=True) * (1.0 / width) + eps)
        inv_s[here, :] = jnp.broadcast_to(inv, (tokens, HEAD_DIM))

    def normalise(i, h):
        here = slice(i * tokens, (i + 1) * tokens)
        piece = x_ref[i, :, head(h)].astype(F32)
        normed = (piece * inv_s[here, :] * gain(h)).astype(BF16)
        normed_s[here, head(h)] = normed
        out_rows[h // (2 * nz), h % 2, here, head((h // 2) % nz)] = normed
        rows = slice((h % GROUP) * tokens, (h % GROUP + 1) * tokens)
        query_s[i, h // GROUP, rows, :] = rotate(normed.astype(F32)).astype(BF16)

    first_moves(2)
    first_moves(0)
    first_moves(1)
    mean_square(0)
    row_arrival(2)
    for t in range(1, long_way + 1):
        for src in range(2):
            for d in range(2):
                ring_arrival(2, src, d, t)
        if t == 1:
            row_arrival(0)
            mean_square(1)
    shared_arrivals(2)
    waiting = [(i, h) for i in range(batches) for h in range(heads)]
    share_of = -(-len(waiting) // (2 * long_way))

    def some_work():
        for _ in range(min(share_of, len(waiting))):
            normalise(*waiting.pop(0))

    for t in range(1, long_way + 1):
        for d in range(2):
            ring_arrival(0, 0, d, t)
            ring_arrival(1, 0, d, t)
        some_work()
        for d in range(2):
            ring_arrival(0, 1, d, t)
            if t > 1 or d == 0:
                cross_arrival(d, t - 1)
        some_work()
    while waiting:
        some_work()
    for d in range(2):
        cross_arrival(d, long_way)
    shared_arrivals(0)
    shared_arrivals(1)
    wk, wv = fk.reshape(width, kv_width), fv.reshape(width, kv_width)

    near = ((xh, 1 - c), (1 - xh, c), (1 - xh, 1 - c))
    row_peers = (partner, across, corner)

    def row_copy(n):
        return remote(
            out_rows.at[near[n][0], near[n][1]], rows_all.at[xh, c], ns.at[n], nr.at[n], row_peers[n]
        )

    rows_all[xh, c] = out_rows[xh, c]

    @pl.when(section < sections - 2)
    def _():
        for n in range(3):
            row_copy(n).start()

    key_pre = nn(normed_s[...], wk[...])
    value_pre = nn(normed_s[...], wv[...])
    pre_k[...] = key_pre
    pre_v[...] = value_pre
    m_at = lax.broadcasted_iota(jnp.int32, (tokens, GROUP * tokens), 0)
    l_at = lax.rem(lax.broadcasted_iota(jnp.int32, (tokens, GROUP * tokens), 1), tokens)
    causal = m_at <= l_at
    for i in range(batches):
        here = slice(i * tokens, (i + 1) * tokens)
        for k in range(KV_HEADS):
            key_s[i, k] = rotate(key_pre[here, head(k)]).astype(BF16)
            value_s[i, k] = value_pre[here, head(k)].astype(BF16)
            scores = nt(key_s[i, k], query_s[i, k]) * scale
            raised = jnp.where(causal, jnp.exp(scores), 0.0)
            prob_s[i, k] = raised / jnp.sum(raised, axis=0, keepdims=True)

    piece_width = width // PIECES
    piece_heads = heads // PIECES

    @pl.when(section == sections - 1)
    def _():
        up_ref[...] = cot_ref[...]

    def piece(ref, i, j):
        return ref.at[i, :, pl.ds(j * piece_width, piece_width)]

    def outgoing(i, j):
        if j in DETOUR:
            n = DETOUR.index(j)
            return remote(piece(low_s, i, j), via_ref.at[i, n], us.at[i, j], vr.at[i, n], two_below)
        return remote(piece(low_s, i, j), piece(up_ref, i, j), us.at[i, j], ur.at[i, j], below)

    def onward(i, n):
        return remote(
            via_ref.at[i, n], piece(up_ref, i, DETOUR[n]), fs.at[i, n], ur.at[i, DETOUR[n]], above
        )

    def pass_on(i):
        for n in range(len(DETOUR)):
            remote(via_ref.at[i, n], via_ref.at[i, n], fs.at[i, n], vr.at[i, n], above).wait_recv()
            onward(i, n).start()

    def kv_copy(i, n):
        peer = (partner, across)[n]
        return remote(kv_s.at[i], kv_all.at[xh, c, i], ks.at[i, n], kr.at[i, n], peer)

    @pl.when(section < sections - 2)
    def _():
        for i in range(batches):
            pass_on(i)

    def one_batch(i, carry):
        start = pl.multiple_of(i * tokens, tokens)
        here = pl.ds(start, tokens)
        inv = inv_s[here, :]
        mean = jnp.zeros((tokens, HEAD_DIM), F32)
        for k in KEY_ORDER:

            @pl.when(section < sections - 1)
            def _():
                for j in (2 * k, 2 * k + 1):
                    slot = piece(up_ref, i, j)
                    remote(slot, slot, us.at[i, j], ur.at[i, j], below).wait_recv()

            upper = jnp.concatenate(
                [up_ref[i, :, head(k * GROUP + h)] for h in range(GROUP)], axis=0
            )
            prob = prob_s[i, k]
            grad_prob = nt(value_s[i, k], upper)
            grad_value = nn(prob.astype(BF16), upper).astype(BF16)
            row_dot = jnp.sum(prob * grad_prob, axis=0, keepdims=True)
            grad_score = (prob * (grad_prob - row_dot) * scale).astype(BF16)
            grad_query = tn(grad_score, key_s[i, k])
            key_back = unrotate(nn(grad_score, query_s[i, k])).astype(BF16)
            kv_s[i, :, head(k)] = key_back
            kv_s[i, :, head(KV_HEADS + k)] = grad_value
            mean = mean + key_back.astype(F32) * pre_k[here, head(k)]
            mean = mean + grad_value.astype(F32) * pre_v[here, head(k)]
            for h in range(GROUP):
                at = head(k * GROUP + h)
                query_back = unrotate(grad_query[h * tokens : (h + 1) * tokens, :])
                qb_s[i, :, at] = query_back
                mean = mean + query_back * (
                    x_ref[i, :, at].astype(F32) * inv * gain(k * GROUP + h)
                )
        row_mean = jnp.sum(mean, axis=-1, keepdims=True) * (1.0 / width)
        drop = inv * inv * row_mean
        key_flat = kv_s[i, :, 0:kv_width]
        value_flat = kv_s[i, :, kv_width : 2 * kv_width]
        for j in SEND_ORDER:
            cols = slice(j * piece_width, (j + 1) * piece_width)
            projected = nt(key_flat, wk[cols, :]) + nt(value_flat, wv[cols, :])
            for h in range(piece_heads):
                at = head(j * piece_heads + h)
                grad_normed = qb_s[i, :, at] + projected[:, head(h)]
                qb_s[i, :, at] = grad_normed
                low_s[i, :, at] = (
                    up_ref[i, :, at].astype(F32)
                    + inv * gain(j * piece_heads + h) * grad_normed
                    - x_ref[i, :, at].astype(F32) * drop
                ).astype(BF16)

            @pl.when(section > 0)
            def _():
                outgoing(i, j).start()

        @pl.when(section == 0)
        def _():
            for n in range(2):
                kv_copy(i, n).start()

        return carry

    lax.fori_loop(0, batches, one_batch, 0)

    @pl.when(section > 0)
    def _():
        for i in range(batches):
            for n in range(2):
                kv_copy(i, n).start()

    @pl.when(section >= sections - 2)
    def _():
        for n in range(3):
            row_copy(n).start()

    @pl.when(section == sections - 1)
    def _():
        for i in range(batches):
            pass_on(i)

    columns = []
    for h in range(heads):
        at = head(h)
        total = jnp.zeros((8, HEAD_DIM), F32)
        for i in range(batches):
            here = slice(i * tokens, (i + 1) * tokens)
            term = qb_s[i, :, at] * x_ref[i, :, at].astype(F32) * inv_s[here, :]
            total = total + jnp.sum(term.reshape(tokens // 8, 8, HEAD_DIM), axis=0)
        columns.append(jnp.sum(total, axis=0, keepdims=True))
    lines = [
        jnp.concatenate([columns[a * 2 * nz + 2 * zz + b] for zz in range(nz)], axis=1)
        for a in range(2)
        for b in range(2)
    ]
    lines.append(jnp.zeros((12, nz * HEAD_DIM), F32))
    col_s[...] = jnp.concatenate(lines, axis=0).astype(BF16)
    kv_all[xh, c] = kv_s[...]
    col_all[xh, c] = col_s[...]
    for n, peer in enumerate((partner, across)):
        push(remote(col_s, col_all.at[xh, c], cs.at[n], cr.at[n], peer))
    for i in range(batches):
        slot = kv_all.at[1 - xh, c, i]
        remote(slot, slot, ks.at[i, 1], kr.at[i, 1], across).wait_recv()
        push(remote(slot, slot, ks.at[i, 2], kr.at[i, 2], partner))
    slot = col_all.at[1 - xh, c]
    remote(slot, slot, cs.at[1], cr.at[1], across).wait_recv()
    push(remote(slot, slot, cs.at[2], cr.at[2], partner))
    for n in range(3):
        slot = rows_all.at[near[n][0], near[n][1]]
        remote(slot, slot, ns.at[n], nr.at[n], row_peers[n]).wait_recv()
    for n, a in ((0, xh), (2, 1 - xh)):
        for i in range(batches):
            slot = kv_all.at[a, 1 - c, i]
            remote(slot, slot, ks.at[i, n], kr.at[i, n], partner).wait_recv()
        slot = col_all.at[a, 1 - c]
        remote(slot, slot, cs.at[n], cr.at[n], partner).wait_recv()

    total_rows = 4 * batches * tokens

    def partial(target, p):
        at = pl.ds(pl.multiple_of(target * HEAD_DIM, HEAD_DIM), HEAD_DIM)
        left = rows_all[:, :, :, at].reshape(total_rows, HEAD_DIM)
        right = kv_all[:, :, :, :, p * kv_width : (p + 1) * kv_width].reshape(total_rows, kv_width)
        return tn(left, right)

    depth = HEAD_DIM // SUBS

    def sum_copy(d, p, t, s):
        return remote(
            sbuf.at[d, p, t, s], rbuf.at[d, p, t, s], rs.at[d, p, t, s], rr.at[d, p, t, s], toward[d]
        )

    for t in range(long_way):
        for p in range(2):
            for d in range(2):
                if t >= hops[p][d]:
                    continue
                steps = hops[p][d] - t
                target = lax.rem(z + (steps if d == 0 else nz - steps), nz)
                mine = partial(target, p)
                for s in range(SUBS):
                    block = mine[s * depth : (s + 1) * depth, :]
                    if t > 0:
                        sum_copy(d, p, t - 1, s).wait_recv()
                        block = block + rbuf[d, p, t - 1, s].astype(F32)
                    sbuf[d, p, t, s] = block.astype(BF16)
                    push(sum_copy(d, p, t, s))
        if t == 0:
            own = lax.broadcasted_iota(jnp.int32, (16, nz * HEAD_DIM), 0) == xh * 2 + c
            totals = jnp.zeros((16, nz * HEAD_DIM), F32)
            for a in range(2):
                for b in range(2):
                    totals = totals + col_all[a, b].astype(F32)
            line = jnp.sum(jnp.where(own, totals, 0.0), axis=0, keepdims=True)
            for zz in range(nz):
                gsend[zz] = jnp.broadcast_to(line[:, head(zz)], (8, HEAD_DIM))
            for s in range(1, nz):
                push(
                    remote(
                        gsend.at[lax.rem(z + s, nz)], grecv.at[s - 1], gs.at[s - 1], gr.at[s - 1],
                        ring[s - 1],
                    )
                )
            for n in range(batches):
                first = plan_ref[n : n + 1, :] == 0
                for h in range(heads):
                    low_out[n, :, head(h)] = jnp.where(
                        first, low_s[0, :, head(h)].astype(F32), low_s[1, :, head(h)].astype(F32)
                    ).astype(BF16)
    outs = (key_out, value_out)
    for p in range(2):
        mine = partial(z, p)
        for s in range(SUBS):
            block = mine[s * depth : (s + 1) * depth, :]
            for d in range(2):
                last = hops[p][d] - 1
                sum_copy(d, p, last, s).wait_recv()
                block = block + rbuf[d, p, last, s].astype(F32)
            outs[p][s * depth : (s + 1) * depth, :] = block
    column = gsend[z]
    for s in range(1, nz):
        remote(gsend.at[0], grecv.at[s - 1], gs.at[s - 1], gr.at[s - 1], ring[s - 1]).wait_recv()
        column = column + grecv[s - 1]
    gain_out[...] = column

    for copy in sends:
        copy.wait_send()
    for n in range(3):
        row_copy(n).wait_send()
    for i in range(batches):
        for n in range(2):
            kv_copy(i, n).wait_send()

    @pl.when(section > 0)
    def _():
        for i in range(batches):
            for j in range(PIECES):
                outgoing(i, j).wait_send()

    @pl.when(section != sections - 2)
    def _():
        for i in range(batches):
            for n in range(len(DETOUR)):
                onward(i, n).wait_send()


def whole(x, cot, wk, wv, gain, plan, ny, nz):
    batches, tokens, width = x.shape
    depth, kv_width = wk.shape
    cosine, sine = rope_tables(tokens, HEAD_DIM)
    rows = batches * tokens
    half = nz // 2
    hop_ring = (2, 2, half, SUBS)
    dma = pltpu.SemaphoreType.DMA
    both = lambda *shape: [dma(shape), dma(shape)]
    via = len(DETOUR)
    return pl.pallas_call(
        functools.partial(kernel, ny, nz),
        out_shape=[
            jax.ShapeDtypeStruct((batches, tokens, width), BF16),
            jax.ShapeDtypeStruct((depth, kv_width), F32),
            jax.ShapeDtypeStruct((depth, kv_width), F32),
            jax.ShapeDtypeStruct((8, depth), F32),
        ],
        in_specs=[pl.BlockSpec(memory_space=pltpu.VMEM)] * 8,
        out_specs=[pl.BlockSpec(memory_space=pltpu.VMEM)] * 4,
        scratch_shapes=[
            pltpu.VMEM((2, nz, 2, depth, kv_width), BF16),
            pltpu.VMEM((2, nz, 2, depth, kv_width), BF16),
            pltpu.VMEM((2, nz, 2, 8, depth), F32),
            pltpu.VMEM((batches, tokens, width), BF16),
            pltpu.VMEM((batches, tokens, width), BF16),
            pltpu.VMEM((batches, via, tokens, width // PIECES), BF16),
            pltpu.VMEM((rows, width), BF16),
            pltpu.VMEM((2, 2, rows, nz * HEAD_DIM), BF16),
            pltpu.VMEM((2, 2, rows, nz * HEAD_DIM), BF16),
            pltpu.VMEM((batches, KV_HEADS, tokens, HEAD_DIM), BF16),
            pltpu.VMEM((batches, KV_HEADS, tokens, HEAD_DIM), BF16),
            pltpu.VMEM((batches, KV_HEADS, GROUP * tokens, HEAD_DIM), BF16),
            pltpu.VMEM((batches, KV_HEADS, tokens, GROUP * tokens), F32),
            pltpu.VMEM((rows, HEAD_DIM), F32),
            pltpu.VMEM((batches, tokens, width), F32),
            pltpu.VMEM((rows, kv_width), F32),
            pltpu.VMEM((rows, kv_width), F32),
            pltpu.VMEM((batches, tokens, 2 * kv_width), BF16),
            pltpu.VMEM((2, 2, batches, tokens, 2 * kv_width), BF16),
            pltpu.VMEM((16, nz * HEAD_DIM), BF16),
            pltpu.VMEM((2, 2, 16, nz * HEAD_DIM), BF16),
            pltpu.VMEM((*hop_ring, depth // SUBS, kv_width), BF16),
            pltpu.VMEM((*hop_ring, depth // SUBS, kv_width), BF16),
            pltpu.VMEM((nz, 8, HEAD_DIM), F32),
            pltpu.VMEM((nz - 1, 8, HEAD_DIM), F32),
            *both(3),
            *both(2, half, 2, 3),
            *both(1 + 2 * half),
            *both(3, 2, 1 + 2 * half),
            *both(batches, PIECES),
            *both(batches, via),
            dma((batches, via)),
            *both(3),
            *both(batches, 3),
            *both(3),
            *both(*hop_ring),
            *both(nz - 1),
        ],
        compiler_params=pltpu.CompilerParams(
            collective_id=0, has_side_effects=True, vmem_limit_bytes=VMEM_LIMIT
        ),
        name="whole",
    )(x, cot, wk, wv, gain, plan, jnp.asarray(cosine), jnp.asarray(sine))


def solution(mesh):
    sections, dp = mesh.shape["section"], mesh.shape["dp"]
    ny, nz = sections // 2, dp // 4
    split = Mesh(mesh.devices.reshape(ny, 2, 2, nz, 2), ("y", "xl", "xh", "z", "c"))

    def body(inputs, cotangent, norm_gain, key_weight, value_weight, plan):
        own_gain = jnp.broadcast_to(norm_gain[0].astype(F32)[None, :], (8, HEAD_DIM))
        order = jnp.broadcast_to(plan[0][:, None], (plan.shape[1], HEAD_DIM))
        low, key_grad, value_grad, gain_grad = whole(
            inputs[0], cotangent, key_weight[0], value_weight[0], own_gain, order, ny, nz
        )
        return low[None], key_grad[None], value_grad[None], gain_grad[0:1]

    placed = (
        P(SECTION, None, DP, None),
        P(None, DP, None),
        P(SECTION, DP),
        P(SECTION, DP, None),
        P(SECTION, DP, None),
        P(SECTION, None),
    )
    return jax.shard_map(
        body,
        mesh=split,
        in_specs=placed,
        out_specs=(
            P(SECTION, None, DP, None),
            P(SECTION, DP, None),
            P(SECTION, DP, None),
            P(SECTION, DP),
        ),
        check_vma=False,
    )
```

time: 239 us -> 204 us (0.85)
  Pallas kernels: 229 us -> 195 us
  other arithmetic: 3.75 us -> 0.01 us
  local copies, waits for them, and re-layouts: 4.78 us -> 7.79 us
    pallas_call x3 -> x1, Pallas kernels: 229 us -> 195 us  [whole(): pl.pallas_call(functools.partial(kernel, ny, nz), out_shape=[jax.ShapeDty...]
    unnamed x8 -> x11, local copies, waits for them, and re-layouts: 1.42 us -> 5.38 us
    reduce_sum x1 -> x0, other arithmetic: 3.01 us -> none  [body(): jnp.sum(jnp.where(selector[:, :, None, None], low[None], jnp.zeros((), BF...]
where the time goes in v2:
time: 204 us
  Pallas kernels  195 us (96%)
  local copies, waits for them, and re-layouts  7.79 us (4%)
    pallas_call x1, Pallas kernels, whole(): pl.pallas_call(functools.partial(kernel, ny, nz), out_shape=[jax.ShapeDty...  195 us
    unnamed x11, local copies, waits for them, and re-layouts  5.38 us

profile of v2, /device:TPU:1, one launch (start us, length us, event | category | flops | bytes accessed | tf_op | source)
XLA Modules:
  0.0 203.6 jit_solution(2470788416140098963)
XLA Ops:
  0.6 0.0 copy-start.2
  0.6 0.6 copy-done.2
  1.3 0.0 copy-start.3
  1.3 0.7 copy-done.3
  1.9 0.6 broadcast_in_dim.31.plan_ref
  2.6 0.6 broadcast_in_dim.29.gain_ref
  3.2 195.1 %whole.1 = (bf16[2,64,4096]{2,1,0:T(8,128)(2,1)}, f32[128,512]{1,0:T(8,128)}, f32[128,512]{1,0:T(8,128)}, f32[8,128]{1,0:T(8,128)}) custom-call(bf16[2,64,4096]{2,1,0:T(8,128)(2,1)} %bitcast.10, bf16[2,64,4096]{2,1,0:T(8,128)(2,1)} %cot_ref.1, bf16[128,512]{1,0:T(8,128)(2,1)} %bitcast.14, bf16[128,512]{1,0:T(8,128)(2,1)} %bitcast.15, ...), custom_call_target="tpu_custom_call" | custom-call | tf_op jit(solution)/shard_map/whole/pallas_call | solution.py:522
  198.3 1.2 slice.3
  199.5 0.0 copy-start.1
  199.5 2.3 %copy.15 = bf16[1,2,64,4096]{3,2,1,0:T(8,128)(2,1)} copy(bf16[1,2,64,4096]{3,2,1,0:T(8,128)(2,1)} %bitcast.11) | data formatting | bytes 2097152
  201.8 0.0 copy-done.1
  201.8 0.0 copy-start
  201.8 0.7 copy.16
  202.5 0.3 copy-done
  202.9 0.7 copy.17
  (1 shorter events, 0.0 us)
Async XLA Ops:
  0.6 0.7 copy-start.2
  1.3 0.7 copy-start.3
  199.5 2.3 %copy-start.1 = (f32[128,512]{1,0:T(8,128)S(1)}, f32[128,512]{1,0:T(8,128)}, u32[]{:S(2)}) copy-start(f32[128,512]{1,0:T(8,128)} %get-tuple-element.9) | copy-start | bytes 786436
  201.8 1.0 copy-start

commit v3 on v2

--- a/solution.py
+++ b/solution.py
@@ -23,8 +23,9 @@
 BF16 = jnp.bfloat16
 
 PIECES = 8
-DETOUR = (0, 1, 2)
-SEND_ORDER = (0, 4, 1, 5, 2, 6, 7, 3)
+DETOUR = (0, 1, 2, 3)
+ALWAYS = (0, 1)
+SEND_ORDER = (0, 4, 1, 5, 6, 2, 7, 3)
 KEY_ORDER = (2, 3, 0, 1)
 SUBS = 2
 
@@ -67,9 +68,9 @@
     ny, nz,
     x_ref, cot_ref, wk_ref, wv_ref, gain_ref, plan_ref, cos_ref, sin_ref,
     low_out, key_out, value_out, gain_out,
-    fk, fv, fg, up_ref, low_s, via_ref, normed_s, out_rows, rows_all, key_s, value_s, query_s,
+    fk, fv, fg, gown, up_ref, low_s, via_ref, normed_s, out_rows, rows_all, key_s, value_s, query_s,
     prob_s, inv_s, qb_s, pre_k, pre_v, kv_s, kv_all, col_s, col_all, sbuf, rbuf, gsend, grecv,
-    xs, xr, zs, zr, ws, wr, ds, dr,
+    xs, xr, zs, zr, ws, wr, ds, dr, ls, lr, bs, br,
     us, ur, vs, vr, fs, ns, nr, ks, kr, cs, cr, rs, rr, gs, gr,
 ):
     y, xl = lax.axis_index("y"), lax.axis_index("xl")
@@ -91,6 +92,7 @@
     toward = (ring[0], ring[nz - 2])
     long_way, short_way = nz // 2, nz - 1 - nz // 2
 
+    gown[...] = jnp.broadcast_to(gain_ref[...].astype(F32), gown.shape)
     barrier = pltpu.get_barrier_semaphore()
     greeted = [across, partner, corner, below, above, two_below, two_above] + ring
     for peer in greeted:
@@ -112,10 +114,10 @@
         return v * cosine - pltpu.roll(v, HEAD_DIM // 2, axis=1) * sine
 
     def gain(h):
-        return fg[h // (2 * nz), (h // 2) % nz, h % 2, 0:1, :]
-
-    sources, fulls = (wk_ref, wv_ref, gain_ref), (fk, fv, fg)
-    hops = ((long_way, short_way), (short_way, long_way), (long_way, short_way))
+        return fg[h // (2 * nz), h % 2, (h // 2) % nz, 0:1, :]
+
+    sources, fulls = (wk_ref, wv_ref), (fk, fv)
+    hops = ((long_way, short_way), (short_way, long_way))
 
     def place(p, src, steps, core=c):
         row = xh if src == 0 else 1 - xh
@@ -135,14 +137,14 @@
 
     def first_moves(p):
         slot = place(p, 0, 0)
-        if p != 1:
-            push(remote(sources[p], slot, xs.at[p], xr.at[p], across))
-        else:
-            push(remote(sources[p], slot, ws.at[0], wr.at[0], across))
         for d in range(2):
             push(ring_copy(sources[p], slot, d, 0, 0, p))
         share(p, 0, sources[p], slot, 0)
         fulls[p][xh, z, c] = sources[p][...]
+
+    def gain_block(row, core, n, peer):
+        slot = fg.at[row, core]
+        return remote(slot, slot, bs.at[n], br.at[n], peer)
 
     def row_arrival(p):
         slot = place(p, 1, 0)
@@ -199,21 +201,22 @@
         rows = slice((h % GROUP) * tokens, (h % GROUP + 1) * tokens)
         query_s[i, h // GROUP, rows, :] = rotate(normed.astype(F32)).astype(BF16)
 
-    first_moves(2)
+    for n in range(1, nz):
+        push(remote(gown, fg.at[xh, c, z], ls.at[n - 1], lr.at[n - 1], ring[n - 1]))
     first_moves(0)
     first_moves(1)
+    fg[xh, c, z] = gown[...]
     mean_square(0)
-    row_arrival(2)
-    for t in range(1, long_way + 1):
-        for src in range(2):
-            for d in range(2):
-                ring_arrival(2, src, d, t)
-        if t == 1:
-            row_arrival(0)
-            mean_square(1)
-    shared_arrivals(2)
+    mean_square(1)
+    for n in range(1, nz):
+        slot = fg.at[xh, c, lax.rem(z + nz - n, nz)]
+        remote(slot, slot, ls.at[n - 1], lr.at[n - 1], ring[n - 1]).wait_recv()
+    for n, peer in enumerate((partner, across)):
+        push(gain_block(xh, c, n, peer))
+    push(remote(sources[0], place(0, 0, 0), xs.at[0], xr.at[0], across))
+    push(remote(sources[1], place(1, 0, 0), ws.at[0], wr.at[0], across))
     waiting = [(i, h) for i in range(batches) for h in range(heads)]
-    share_of = -(-len(waiting) // (2 * long_way))
+    share_of = -(-len(waiting) // (2 * long_way - 2))
 
     def some_work():
         for _ in range(min(share_of, len(waiting))):
@@ -223,12 +226,21 @@
         for d in range(2):
             ring_arrival(0, 0, d, t)
             ring_arrival(1, 0, d, t)
-        some_work()
+        if t == 1:
+            row_arrival(0)
+            gain_block(1 - xh, c, 1, across).wait_recv()
+            push(gain_block(1 - xh, c, 2, partner))
+        else:
+            some_work()
         for d in range(2):
             ring_arrival(0, 1, d, t)
             if t > 1 or d == 0:
                 cross_arrival(d, t - 1)
-        some_work()
+        if t == 1:
+            gain_block(xh, 1 - c, 0, partner).wait_recv()
+            gain_block(1 - xh, 1 - c, 2, partner).wait_recv()
+        else:
+            some_work()
     while waiting:
         some_work()
     for d in range(2):
@@ -278,11 +290,25 @@
     def piece(ref, i, j):
         return ref.at[i, :, pl.ds(j * piece_width, piece_width)]
 
-    def outgoing(i, j):
+    def direct(i, j):
+        return remote(piece(low_s, i, j), piece(up_ref, i, j), us.at[i, j], ur.at[i, j], below)
+
+    def roundabout(i, j):
+        n = DETOUR.index(j)
+        return remote(piece(low_s, i, j), via_ref.at[i, n], us.at[i, j], vr.at[i, n], two_below)
+
+    def send_piece(i, j):
         if j in DETOUR:
-            n = DETOUR.index(j)
-            return remote(piece(low_s, i, j), via_ref.at[i, n], us.at[i, j], vr.at[i, n], two_below)
-        return remote(piece(low_s, i, j), piece(up_ref, i, j), us.at[i, j], ur.at[i, j], below)
+
+            @pl.when((section > 0) if j in ALWAYS else (section > 0) & (xl == 0))
+            def _():
+                roundabout(i, j).start()
+
+        if j not in ALWAYS:
+
+            @pl.when((xl == 1) if j in DETOUR else section > 0)
+            def _():
+                direct(i, j).start()
 
     def onward(i, n):
         return remote(
@@ -290,9 +316,15 @@
         )
 
     def pass_on(i):
-        for n in range(len(DETOUR)):
+        def one(n):
             remote(via_ref.at[i, n], via_ref.at[i, n], fs.at[i, n], vr.at[i, n], above).wait_recv()
             onward(i, n).start()
+
+        for n, j in enumerate(DETOUR):
+            if j in ALWAYS:
+                one(n)
+            else:
+                pl.when(xl == 0)(functools.partial(one, n))
 
     def kv_copy(i, n):
         peer = (partner, across)[n]
@@ -354,9 +386,7 @@
                     - x_ref[i, :, at].astype(F32) * drop
                 ).astype(BF16)
 
-            @pl.when(section > 0)
-            def _():
-                outgoing(i, j).start()
+            send_piece(i, j)
 
         @pl.when(section == 0)
         def _():
@@ -467,7 +497,7 @@
                     )
                 )
             for n in range(batches):
-                first = plan_ref[n : n + 1, :] == 0
+                first = plan_ref[0, n] == 0
                 for h in range(heads):
                     low_out[n, :, head(h)] = jnp.where(
                         first, low_s[0, :, head(h)].astype(F32), low_s[1, :, head(h)].astype(F32)
@@ -486,7 +516,7 @@
     for s in range(1, nz):
         remote(gsend.at[0], grecv.at[s - 1], gs.at[s - 1], gr.at[s - 1], ring[s - 1]).wait_recv()
         column = column + grecv[s - 1]
-    gain_out[...] = column
+    gain_out[...] = column[0:1, :]
 
     for copy in sends:
         copy.wait_send()
@@ -500,12 +530,18 @@
     def _():
         for i in range(batches):
             for j in range(PIECES):
-                outgoing(i, j).wait_send()
+                direct(i, j).wait_send()
 
     @pl.when(section != sections - 2)
     def _():
         for i in range(batches):
-            for n in range(len(DETOUR)):
+            for n in range(len(ALWAYS)):
+                onward(i, n).wait_send()
+
+    @pl.when((section < sections - 2) & (xl == 0))
+    def _():
+        for i in range(batches):
+            for n in range(len(ALWAYS), len(DETOUR)):
                 onward(i, n).wait_send()
 
 
@@ -525,14 +561,17 @@
             jax.ShapeDtypeStruct((batches, tokens, width), BF16),
             jax.ShapeDtypeStruct((depth, kv_width), F32),
             jax.ShapeDtypeStruct((depth, kv_width), F32),
-            jax.ShapeDtypeStruct((8, depth), F32),
+            jax.ShapeDtypeStruct((1, depth), F32),
         ],
-        in_specs=[pl.BlockSpec(memory_space=pltpu.VMEM)] * 8,
+        in_specs=[pl.BlockSpec(memory_space=pltpu.VMEM)] * 5
+        + [pl.BlockSpec(memory_space=pltpu.SMEM)]
+        + [pl.BlockSpec(memory_space=pltpu.VMEM)] * 2,
         out_specs=[pl.BlockSpec(memory_space=pltpu.VMEM)] * 4,
         scratch_shapes=[
             pltpu.VMEM((2, nz, 2, depth, kv_width), BF16),
             pltpu.VMEM((2, nz, 2, depth, kv_width), BF16),
-            pltpu.VMEM((2, nz, 2, 8, depth), F32),
+            pltpu.VMEM((2, 2, nz, 8, depth), F32),
+            pltpu.VMEM((8, depth), F32),
             pltpu.VMEM((batches, tokens, width), BF16),
             pltpu.VMEM((batches, tokens, width), BF16),
             pltpu.VMEM((batches, via, tokens, width // PIECES), BF16),
@@ -555,10 +594,12 @@
             pltpu.VMEM((*hop_ring, depth // SUBS, kv_width), BF16),
             pltpu.VMEM((nz, 8, HEAD_DIM), F32),
             pltpu.VMEM((nz - 1, 8, HEAD_DIM), F32),
+            *both(1),
+            *both(2, half, 2, 2),
+            *both(1 + 2 * half),
+            *both(2, 2, 1 + 2 * half),
+            *both(nz - 1),
             *both(3),
-            *both(2, half, 2, 3),
-            *both(1 + 2 * half),
-            *both(3, 2, 1 + 2 * half),
             *both(batches, PIECES),
             *both(batches, via),
             dma((batches, via)),
@@ -581,12 +622,10 @@
     split = Mesh(mesh.devices.reshape(ny, 2, 2, nz, 2), ("y", "xl", "xh", "z", "c"))
 
     def body(inputs, cotangent, norm_gain, key_weight, value_weight, plan):
-        own_gain = jnp.broadcast_to(norm_gain[0].astype(F32)[None, :], (8, HEAD_DIM))
-        order = jnp.broadcast_to(plan[0][:, None], (plan.shape[1], HEAD_DIM))
         low, key_grad, value_grad, gain_grad = whole(
-            inputs[0], cotangent, key_weight[0], value_weight[0], own_gain, order, ny, nz
+            inputs[0], cotangent, key_weight[0], value_weight[0], norm_gain, plan, ny, nz
         )
-        return low[None], key_grad[None], value_grad[None], gain_grad[0:1]
+        return low[None], key_grad[None], value_grad[None], gain_grad
 
     placed = (
         P(SECTION, None, DP, None),

time: 204 us -> 189 us (0.926)
  Pallas kernels: 195 us -> 183 us
  local copies, waits for them, and re-layouts: 7.79 us -> 4.59 us
    pallas_call x1, Pallas kernels: 195 us -> 183 us  [whole(): pl.pallas_call(functools.partial(kernel, ny, nz), out_shape=[jax.ShapeDty...]
    unnamed x11 -> x10, local copies, waits for them, and re-layouts: 5.38 us -> 4.59 us
where the time goes in v3:
time: 189 us
  Pallas kernels  183 us (97%)
  local copies, waits for them, and re-layouts  4.59 us (2%)
    pallas_call x1, Pallas kernels, whole(): pl.pallas_call(functools.partial(kernel, ny, nz), out_shape=[jax.ShapeDty...  183 us
    unnamed x10, local copies, waits for them, and re-layouts  4.59 us

profile of v3, /device:TPU:1, one launch (start us, length us, event | category | flops | bytes accessed | tf_op | source)
XLA Modules:
  0.0 188.6 jit_solution(13855872214575737965)
XLA Ops:
  0.6 183.4 %whole.1 = (bf16[2,64,4096]{2,1,0:T(8,128)(2,1)}, f32[128,512]{1,0:T(8,128)}, f32[128,512]{1,0:T(8,128)}, f32[1,128]{1,0:T(1,128)}) custom-call(bf16[2,64,4096]{2,1,0:T(8,128)(2,1)} %bitcast.6, bf16[2,64,4096]{2,1,0:T(8,128)(2,1)} %cot_ref.1, bf16[128,512]{1,0:T(8,128)(2,1)} %bitcast.10, bf16[128,512]{1,0:T(8,128)(2,1)} %bitcast.11, ...), custom_call_target="tpu_custom_call" | custom-call | tf_op jit(solution)/shard_map/whole/pallas_call | solution.py:558
  184.0 0.0 copy-start.1
  184.0 2.3 %copy.16 = bf16[1,2,64,4096]{3,2,1,0:T(8,128)(2,1)} copy(bf16[1,2,64,4096]{3,2,1,0:T(8,128)(2,1)} %bitcast.7) | data formatting | bytes 2097152
  186.3 0.0 copy-done.1
  186.4 0.0 copy-start
  186.4 0.7 copy.17
  187.1 0.3 copy-done
  187.4 0.0 copy-start.2
  187.4 0.7 copy.18
  188.1 0.0 copy-done.2
  188.1 0.5 copy.19
Async XLA Ops:
  184.0 2.3 %copy-start.1 = (f32[128,512]{1,0:T(8,128)S(1)}, f32[128,512]{1,0:T(8,128)}, u32[]{:S(2)}) copy-start(f32[128,512]{1,0:T(8,128)} %get-tuple-element.9) | copy-start | bytes 786436
  186.4 1.0 copy-start
  187.4 0.7 copy-start.2

commit v4 on v3

--- a/solution.py
+++ b/solution.py
@@ -23,9 +23,11 @@
 BF16 = jnp.bfloat16
 
 PIECES = 8
-DETOUR = (0, 1, 2, 3)
-ALWAYS = (0, 1)
-SEND_ORDER = (0, 4, 1, 5, 6, 2, 7, 3)
+EVEN_DOWN = (0, 1, 2, 3)
+ODD_DOWN = (0,)
+ODD_UP = (2, 3)
+DOWN = tuple(sorted(set(EVEN_DOWN + ODD_DOWN)))
+SEND_ORDER = (0, 4, 1, 5, 2, 6, 3, 7)
 KEY_ORDER = (2, 3, 0, 1)
 SUBS = 2
 
@@ -68,10 +70,10 @@
     ny, nz,
     x_ref, cot_ref, wk_ref, wv_ref, gain_ref, plan_ref, cos_ref, sin_ref,
     low_out, key_out, value_out, gain_out,
-    fk, fv, fg, gown, up_ref, low_s, via_ref, normed_s, out_rows, rows_all, key_s, value_s, query_s,
-    prob_s, inv_s, qb_s, pre_k, pre_v, kv_s, kv_all, col_s, col_all, sbuf, rbuf, gsend, grecv,
+    fk, fv, fg, gown, up_ref, low_s, via_ref, hill_ref, normed_s, out_rows, rows_all, key_s, value_s, query_s,
+    prob_s, inv_s, drop_s, qb_s, pre_k, pre_v, kv_s, kv_all, col_s, col_all, sbuf, rbuf, gsend, grecv,
     xs, xr, zs, zr, ws, wr, ds, dr, ls, lr, bs, br,
-    us, ur, vs, vr, fs, ns, nr, ks, kr, cs, cr, rs, rr, gs, gr,
+    us, ur, vs, vr, fs, hs, hr, ns, nr, ks, kr, cs, cr, rs, rr, gs, gr,
 ):
     y, xl = lax.axis_index("y"), lax.axis_index("xl")
     xh, z, c = lax.axis_index("xh"), lax.axis_index("z"), lax.axis_index("c")
@@ -87,6 +89,7 @@
 
     below, above = section_peer(-1), section_peer(1)
     two_below, two_above = section_peer(-2), section_peer(2)
+    three_below, three_above = section_peer(-3), section_peer(3)
     across, partner, corner = {"xh": 1 - xh}, {"c": 1 - c}, {"xh": 1 - xh, "c": 1 - c}
     ring = [{"z": lax.rem(z + s, nz)} for s in range(1, nz)]
     toward = (ring[0], ring[nz - 2])
@@ -94,7 +97,8 @@
 
     gown[...] = jnp.broadcast_to(gain_ref[...].astype(F32), gown.shape)
     barrier = pltpu.get_barrier_semaphore()
-    greeted = [across, partner, corner, below, above, two_below, two_above] + ring
+    greeted = [across, partner, corner, below, above, two_below, two_above]
+    greeted += [three_below, three_above] + ring
     for peer in greeted:
         pl.semaphore_signal(barrier, inc=1, device_id=peer, device_id_type=MESH_ID)
     pl.semaphore_wait(barrier, len(greeted))
@@ -206,17 +210,20 @@
     first_moves(0)
     first_moves(1)
     fg[xh, c, z] = gown[...]
+    push(remote(sources[0], place(0, 0, 0), xs.at[0], xr.at[0], across))
+    push(remote(sources[1], place(1, 0, 0), ws.at[0], wr.at[0], across))
     mean_square(0)
     mean_square(1)
-    for n in range(1, nz):
-        slot = fg.at[xh, c, lax.rem(z + nz - n, nz)]
-        remote(slot, slot, ls.at[n - 1], lr.at[n - 1], ring[n - 1]).wait_recv()
-    for n, peer in enumerate((partner, across)):
-        push(gain_block(xh, c, n, peer))
-    push(remote(sources[0], place(0, 0, 0), xs.at[0], xr.at[0], across))
-    push(remote(sources[1], place(1, 0, 0), ws.at[0], wr.at[0], across))
+
+    def own_gains():
+        for n in range(1, nz):
+            slot = fg.at[xh, c, lax.rem(z + nz - n, nz)]
+            remote(slot, slot, ls.at[n - 1], lr.at[n - 1], ring[n - 1]).wait_recv()
+        for n, peer in enumerate((partner, across)):
+            push(gain_block(xh, c, n, peer))
+
     waiting = [(i, h) for i in range(batches) for h in range(heads)]
-    share_of = -(-len(waiting) // (2 * long_way - 2))
+    share_of = -(-len(waiting) // (2 * long_way - 4))
 
     def some_work():
         for _ in range(min(share_of, len(waiting))):
@@ -228,6 +235,8 @@
             ring_arrival(1, 0, d, t)
         if t == 1:
             row_arrival(0)
+            own_gains()
+        elif t == 2:
             gain_block(1 - xh, c, 1, across).wait_recv()
             push(gain_block(1 - xh, c, 2, partner))
         else:
@@ -236,10 +245,10 @@
             ring_arrival(0, 1, d, t)
             if t > 1 or d == 0:
                 cross_arrival(d, t - 1)
-        if t == 1:
+        if t == 2:
             gain_block(xh, 1 - c, 0, partner).wait_recv()
             gain_block(1 - xh, 1 - c, 2, partner).wait_recv()
-        else:
+        elif t > 2:
             some_work()
     while waiting:
         some_work()
@@ -264,22 +273,27 @@
         for n in range(3):
             row_copy(n).start()
 
-    key_pre = nn(normed_s[...], wk[...])
-    value_pre = nn(normed_s[...], wv[...])
-    pre_k[...] = key_pre
-    pre_v[...] = value_pre
+    pre_k[...] = nn(normed_s[...], wk[...])
+    pre_v[...] = nn(normed_s[...], wv[...])
     m_at = lax.broadcasted_iota(jnp.int32, (tokens, GROUP * tokens), 0)
     l_at = lax.rem(lax.broadcasted_iota(jnp.int32, (tokens, GROUP * tokens), 1), tokens)
     causal = m_at <= l_at
-    for i in range(batches):
+
+    def attend(i):
         here = slice(i * tokens, (i + 1) * tokens)
         for k in range(KV_HEADS):
-            key_s[i, k] = rotate(key_pre[here, head(k)]).astype(BF16)
-            value_s[i, k] = value_pre[here, head(k)].astype(BF16)
+            key_s[i, k] = rotate(pre_k[here, head(k)]).astype(BF16)
+            value_s[i, k] = pre_v[here, head(k)].astype(BF16)
             scores = nt(key_s[i, k], query_s[i, k]) * scale
             raised = jnp.where(causal, jnp.exp(scores), 0.0)
             prob_s[i, k] = raised / jnp.sum(raised, axis=0, keepdims=True)
 
+    attend(0)
+
+    @pl.when(section < sections - 1)
+    def _():
+        attend(1)
+
     piece_width = width // PIECES
     piece_heads = heads // PIECES
 
@@ -294,46 +308,83 @@
         return remote(piece(low_s, i, j), piece(up_ref, i, j), us.at[i, j], ur.at[i, j], below)
 
     def roundabout(i, j):
-        n = DETOUR.index(j)
+        n = DOWN.index(j)
         return remote(piece(low_s, i, j), via_ref.at[i, n], us.at[i, j], vr.at[i, n], two_below)
 
+    def uphill(i, j):
+        n = ODD_UP.index(j)
+        return remote(piece(low_s, i, j), hill_ref.at[i, n], us.at[i, j], hr.at[i, n], two_above)
+
+    def over(i, n):
+        j = ODD_UP[n]
+        return remote(hill_ref.at[i, n], piece(up_ref, i, j), hs.at[i, n], ur.at[i, j], three_below)
+
+    def hand_down(i):
+        for n in range(len(ODD_UP)):
+            slot = hill_ref.at[i, n]
+            remote(slot, slot, hs.at[i, n], hr.at[i, n], three_below).wait_recv()
+            over(i, n).start()
+
+    def on_parity(even, odd, run, base=None):
+        if even and odd:
+            run() if base is None else pl.when(base)(run)
+        elif even:
+            pl.when((xl == 0) if base is None else (xl == 0) & base)(run)
+        elif odd:
+            pl.when((xl == 1) if base is None else (xl == 1) & base)(run)
+
     def send_piece(i, j):
-        if j in DETOUR:
-
-            @pl.when((section > 0) if j in ALWAYS else (section > 0) & (xl == 0))
-            def _():
-                roundabout(i, j).start()
-
-        if j not in ALWAYS:
-
-            @pl.when((xl == 1) if j in DETOUR else section > 0)
-            def _():
-                direct(i, j).start()
+        on_parity(j in EVEN_DOWN, j in ODD_DOWN, lambda: roundabout(i, j).start(), section > 0)
+        on_parity(False, j in ODD_UP, lambda: uphill(i, j).start())
+        on_parity(
+            j not in EVEN_DOWN, j not in ODD_DOWN + ODD_UP, lambda: direct(i, j).start(), section > 0
+        )
 
     def onward(i, n):
         return remote(
-            via_ref.at[i, n], piece(up_ref, i, DETOUR[n]), fs.at[i, n], ur.at[i, DETOUR[n]], above
+            via_ref.at[i, n], piece(up_ref, i, DOWN[n]), fs.at[i, n], ur.at[i, DOWN[n]], above
         )
 
+    def pass_piece(i, n):
+        remote(via_ref.at[i, n], via_ref.at[i, n], fs.at[i, n], vr.at[i, n], above).wait_recv()
+        onward(i, n).start()
+
     def pass_on(i):
-        def one(n):
-            remote(via_ref.at[i, n], via_ref.at[i, n], fs.at[i, n], vr.at[i, n], above).wait_recv()
-            onward(i, n).start()
-
-        for n, j in enumerate(DETOUR):
-            if j in ALWAYS:
-                one(n)
-            else:
-                pl.when(xl == 0)(functools.partial(one, n))
+        for n, j in enumerate(DOWN):
+            on_parity(j in EVEN_DOWN, j in ODD_DOWN, functools.partial(pass_piece, i, n))
 
     def kv_copy(i, n):
         peer = (partner, across)[n]
         return remote(kv_s.at[i], kv_all.at[xh, c, i], ks.at[i, n], kr.at[i, n], peer)
 
+    @pl.when(section == 1)
+    def _():
+        for i in range(batches):
+            hand_down(i)
+
     @pl.when(section < sections - 2)
     def _():
-        for i in range(batches):
-            pass_on(i)
+        pass_on(0)
+        pass_on(1)
+
+    def project(i, here):
+        inv, drop = inv_s[here, :], drop_s[here, :]
+        key_flat = kv_s[i, :, 0:kv_width]
+        value_flat = kv_s[i, :, kv_width : 2 * kv_width]
+        for j in SEND_ORDER:
+            cols = slice(j * piece_width, (j + 1) * piece_width)
+            projected = nt(key_flat, wk[cols, :]) + nt(value_flat, wv[cols, :])
+            for h in range(piece_heads):
+                at = head(j * piece_heads + h)
+                grad_normed = qb_s[i, :, at] + projected[:, head(h)]
+                qb_s[i, :, at] = grad_normed
+                low_s[i, :, at] = (
+                    up_ref[i, :, at].astype(F32)
+                    + inv * gain(j * piece_heads + h) * grad_normed
+                    - x_ref[i, :, at].astype(F32) * drop
+                ).astype(BF16)
+
+            send_piece(i, j)
 
     def one_batch(i, carry):
         start = pl.multiple_of(i * tokens, tokens)
@@ -344,7 +395,7 @@
 
             @pl.when(section < sections - 1)
             def _():
-                for j in (2 * k, 2 * k + 1):
+                for j in range(k * PIECES // KV_HEADS, (k + 1) * PIECES // KV_HEADS):
                     slot = piece(up_ref, i, j)
                     remote(slot, slot, us.at[i, j], ur.at[i, j], below).wait_recv()
 
@@ -369,30 +420,22 @@
                 mean = mean + query_back * (
                     x_ref[i, :, at].astype(F32) * inv * gain(k * GROUP + h)
                 )
-        row_mean = jnp.sum(mean, axis=-1, keepdims=True) * (1.0 / width)
-        drop = inv * inv * row_mean
-        key_flat = kv_s[i, :, 0:kv_width]
-        value_flat = kv_s[i, :, kv_width : 2 * kv_width]
-        for j in SEND_ORDER:
-            cols = slice(j * piece_width, (j + 1) * piece_width)
-            projected = nt(key_flat, wk[cols, :]) + nt(value_flat, wv[cols, :])
-            for h in range(piece_heads):
-                at = head(j * piece_heads + h)
-                grad_normed = qb_s[i, :, at] + projected[:, head(h)]
-                qb_s[i, :, at] = grad_normed
-                low_s[i, :, at] = (
-                    up_ref[i, :, at].astype(F32)
-                    + inv * gain(j * piece_heads + h) * grad_normed
-                    - x_ref[i, :, at].astype(F32) * drop
-                ).astype(BF16)
-
-            send_piece(i, j)
-
         @pl.when(section == 0)
         def _():
             for n in range(2):
                 kv_copy(i, n).start()
 
+        drop_s[here, :] = inv * inv * (jnp.sum(mean, axis=-1, keepdims=True) * (1.0 / width))
+
+        @pl.when((section > 0) | (i == 0))
+        def _():
+            project(i, here)
+
+        @pl.when((i == 0) & (section == sections - 1))
+        def _():
+            attend(1)
+
+
         return carry
 
     lax.fori_loop(0, batches, one_batch, 0)
@@ -408,38 +451,21 @@
         for n in range(3):
             row_copy(n).start()
 
+    @pl.when((xl == 1) & (section > 1))
+    def _():
+        for i in range(batches):
+            hand_down(i)
+
     @pl.when(section == sections - 1)
     def _():
         for i in range(batches):
             pass_on(i)
 
-    columns = []
-    for h in range(heads):
-        at = head(h)
-        total = jnp.zeros((8, HEAD_DIM), F32)
-        for i in range(batches):
-            here = slice(i * tokens, (i + 1) * tokens)
-            term = qb_s[i, :, at] * x_ref[i, :, at].astype(F32) * inv_s[here, :]
-            total = total + jnp.sum(term.reshape(tokens // 8, 8, HEAD_DIM), axis=0)
-        columns.append(jnp.sum(total, axis=0, keepdims=True))
-    lines = [
-        jnp.concatenate([columns[a * 2 * nz + 2 * zz + b] for zz in range(nz)], axis=1)
-        for a in range(2)
-        for b in range(2)
-    ]
-    lines.append(jnp.zeros((12, nz * HEAD_DIM), F32))
-    col_s[...] = jnp.concatenate(lines, axis=0).astype(BF16)
     kv_all[xh, c] = kv_s[...]
-    col_all[xh, c] = col_s[...]
-    for n, peer in enumerate((partner, across)):
-        push(remote(col_s, col_all.at[xh, c], cs.at[n], cr.at[n], peer))
     for i in range(batches):
         slot = kv_all.at[1 - xh, c, i]
         remote(slot, slot, ks.at[i, 1], kr.at[i, 1], across).wait_recv()
         push(remote(slot, slot, ks.at[i, 2], kr.at[i, 2], partner))
-    slot = col_all.at[1 - xh, c]
-    remote(slot, slot, cs.at[1], cr.at[1], across).wait_recv()
-    push(remote(slot, slot, cs.at[2], cr.at[2], partner))
     for n in range(3):
         slot = rows_all.at[near[n][0], near[n][1]]
         remote(slot, slot, ns.at[n], nr.at[n], row_peers[n]).wait_recv()
@@ -447,8 +473,60 @@
         for i in range(batches):
             slot = kv_all.at[a, 1 - c, i]
             remote(slot, slot, ks.at[i, n], kr.at[i, n], partner).wait_recv()
-        slot = col_all.at[a, 1 - c]
-        remote(slot, slot, cs.at[n], cr.at[n], partner).wait_recv()
+
+    def column_sums():
+        columns = []
+        for h in range(heads):
+            at = head(h)
+            total = jnp.zeros((8, HEAD_DIM), F32)
+            for i in range(batches):
+                here = slice(i * tokens, (i + 1) * tokens)
+                term = qb_s[i, :, at] * x_ref[i, :, at].astype(F32) * inv_s[here, :]
+                total = total + jnp.sum(term.reshape(tokens // 8, 8, HEAD_DIM), axis=0)
+            columns.append(jnp.sum(total, axis=0, keepdims=True))
+        lines = [
+            jnp.concatenate([columns[a * 2 * nz + 2 * zz + b] for zz in range(nz)], axis=1)
+            for a in range(2)
+            for b in range(2)
+        ]
+        lines.append(jnp.zeros((12, nz * HEAD_DIM), F32))
+        col_s[...] = jnp.concatenate(lines, axis=0).astype(BF16)
+        col_all[xh, c] = col_s[...]
+        for n, peer in enumerate((partner, across)):
+            push(remote(col_s, col_all.at[xh, c], cs.at[n], cr.at[n], peer))
+
+    def columns_on():
+        slot = col_all.at[1 - xh, c]
+        remote(slot, slot, cs.at[1], cr.at[1], across).wait_recv()
+        push(remote(slot, slot, cs.at[2], cr.at[2], partner))
+
+    def columns_out():
+        for n, a in ((0, xh), (2, 1 - xh)):
+            slot = col_all.at[a, 1 - c]
+            remote(slot, slot, cs.at[n], cr.at[n], partner).wait_recv()
+        own = lax.broadcasted_iota(jnp.int32, (16, nz * HEAD_DIM), 0) == xh * 2 + c
+        totals = jnp.zeros((16, nz * HEAD_DIM), F32)
+        for a in range(2):
+            for b in range(2):
+                totals = totals + col_all[a, b].astype(F32)
+        line = jnp.sum(jnp.where(own, totals, 0.0), axis=0, keepdims=True)
+        for zz in range(nz):
+            gsend[zz] = jnp.broadcast_to(line[:, head(zz)], (8, HEAD_DIM))
+        for s in range(1, nz):
+            push(
+                remote(
+                    gsend.at[lax.rem(z + s, nz)], grecv.at[s - 1], gs.at[s - 1], gr.at[s - 1],
+                    ring[s - 1],
+                )
+            )
+
+    def write_low():
+        for n in range(batches):
+            first = plan_ref[0, n] == 0
+            for h in range(heads):
+                low_out[n, :, head(h)] = jnp.where(
+                    first, low_s[0, :, head(h)].astype(F32), low_s[1, :, head(h)].astype(F32)
+                ).astype(BF16)
 
     total_rows = 4 * batches * tokens
 
@@ -481,27 +559,17 @@
                     sbuf[d, p, t, s] = block.astype(BF16)
                     push(sum_copy(d, p, t, s))
         if t == 0:
-            own = lax.broadcasted_iota(jnp.int32, (16, nz * HEAD_DIM), 0) == xh * 2 + c
-            totals = jnp.zeros((16, nz * HEAD_DIM), F32)
-            for a in range(2):
-                for b in range(2):
-                    totals = totals + col_all[a, b].astype(F32)
-            line = jnp.sum(jnp.where(own, totals, 0.0), axis=0, keepdims=True)
-            for zz in range(nz):
-                gsend[zz] = jnp.broadcast_to(line[:, head(zz)], (8, HEAD_DIM))
-            for s in range(1, nz):
-                push(
-                    remote(
-                        gsend.at[lax.rem(z + s, nz)], grecv.at[s - 1], gs.at[s - 1], gr.at[s - 1],
-                        ring[s - 1],
-                    )
-                )
-            for n in range(batches):
-                first = plan_ref[0, n] == 0
-                for h in range(heads):
-                    low_out[n, :, head(h)] = jnp.where(
-                        first, low_s[0, :, head(h)].astype(F32), low_s[1, :, head(h)].astype(F32)
-                    ).astype(BF16)
+
+            @pl.when(section == 0)
+            def _():
+                project(batches - 1, slice((batches - 1) * tokens, batches * tokens))
+
+            column_sums()
+        elif t == 1:
+            columns_on()
+            write_low()
+        elif t == 2:
+            columns_out()
     outs = (key_out, value_out)
     for p in range(2):
         mine = partial(z, p)
@@ -535,14 +603,14 @@
     @pl.when(section != sections - 2)
     def _():
         for i in range(batches):
-            for n in range(len(ALWAYS)):
-                onward(i, n).wait_send()
-
-    @pl.when((section < sections - 2) & (xl == 0))
+            for n, j in enumerate(DOWN):
+                on_parity(j in EVEN_DOWN, j in ODD_DOWN, lambda: onward(i, n).wait_send())
+
+    @pl.when(xl == 1)
     def _():
         for i in range(batches):
-            for n in range(len(ALWAYS), len(DETOUR)):
-                onward(i, n).wait_send()
+            for n in range(len(ODD_UP)):
+                over(i, n).wait_send()
 
 
 def whole(x, cot, wk, wv, gain, plan, ny, nz):
@@ -554,7 +622,7 @@
     hop_ring = (2, 2, half, SUBS)
     dma = pltpu.SemaphoreType.DMA
     both = lambda *shape: [dma(shape), dma(shape)]
-    via = len(DETOUR)
+    via = len(DOWN)
     return pl.pallas_call(
         functools.partial(kernel, ny, nz),
         out_shape=[
@@ -575,6 +643,7 @@
             pltpu.VMEM((batches, tokens, width), BF16),
             pltpu.VMEM((batches, tokens, width), BF16),
             pltpu.VMEM((batches, via, tokens, width // PIECES), BF16),
+            pltpu.VMEM((batches, len(ODD_UP), tokens, width // PIECES), BF16),
             pltpu.VMEM((rows, width), BF16),
             pltpu.VMEM((2, 2, rows, nz * HEAD_DIM), BF16),
             pltpu.VMEM((2, 2, rows, nz * HEAD_DIM), BF16),
@@ -582,6 +651,7 @@
             pltpu.VMEM((batches, KV_HEADS, tokens, HEAD_DIM), BF16),
             pltpu.VMEM((batches, KV_HEADS, GROUP * tokens, HEAD_DIM), BF16),
             pltpu.VMEM((batches, KV_HEADS, tokens, GROUP * tokens), F32),
+            pltpu.VMEM((rows, HEAD_DIM), F32),
             pltpu.VMEM((rows, HEAD_DIM), F32),
             pltpu.VMEM((batches, tokens, width), F32),
             pltpu.VMEM((rows, kv_width), F32),
@@ -603,6 +673,7 @@
             *both(batches, PIECES),
             *both(batches, via),
             dma((batches, via)),
+            *both(batches, len(ODD_UP)),
             *both(3),
             *both(batches, 3),
             *both(3),

time: 189 us -> 184 us (0.974)
  Pallas kernels: 183 us -> 179 us
    pallas_call x1, Pallas kernels: 183 us -> 179 us  [whole(): pl.pallas_call(functools.partial(kernel, ny, nz), out_shape=[jax.ShapeDty...]
where the time goes in v4:
time: 184 us
  Pallas kernels  179 us (97%)
  local copies, waits for them, and re-layouts  4.59 us (2%)
    pallas_call x1, Pallas kernels, whole(): pl.pallas_call(functools.partial(kernel, ny, nz), out_shape=[jax.ShapeDty...  179 us
    unnamed x10, local copies, waits for them, and re-layouts  4.59 us

profile of v4, /device:TPU:1, one launch (start us, length us, event | category | flops | bytes accessed | tf_op | source)
XLA Modules:
  0.0 184.0 jit_solution(10591932283296986970)
XLA Ops:
  0.6 178.8 %whole.1 = (bf16[2,64,4096]{2,1,0:T(8,128)(2,1)}, f32[128,512]{1,0:T(8,128)}, f32[128,512]{1,0:T(8,128)}, f32[1,128]{1,0:T(1,128)}) custom-call(bf16[2,64,4096]{2,1,0:T(8,128)(2,1)} %bitcast.6, bf16[2,64,4096]{2,1,0:T(8,128)(2,1)} %cot_ref.1, bf16[128,512]{1,0:T(8,128)(2,1)} %bitcast.10, bf16[128,512]{1,0:T(8,128)(2,1)} %bitcast.11, ...), custom_call_target="tpu_custom_call" | custom-call | tf_op jit(solution)/shard_map/whole/pallas_call | solution.py:626
  179.4 0.0 copy-start.1
  179.4 2.3 %copy.16 = bf16[1,2,64,4096]{3,2,1,0:T(8,128)(2,1)} copy(bf16[1,2,64,4096]{3,2,1,0:T(8,128)(2,1)} %bitcast.7) | data formatting | bytes 2097152
  181.8 0.0 copy-done.1
  181.8 0.0 copy-start
  181.8 0.7 copy.17
  182.5 0.3 copy-done
  182.8 0.0 copy-start.2
  182.8 0.7 copy.18
  183.5 0.0 copy-done.2
  183.5 0.5 copy.19
Async XLA Ops:
  179.4 2.3 %copy-start.1 = (f32[128,512]{1,0:T(8,128)S(1)}, f32[128,512]{1,0:T(8,128)}, u32[]{:S(2)}) copy-start(f32[128,512]{1,0:T(8,128)} %get-tuple-element.9) | copy-start | bytes 786436
  181.8 1.0 copy-start
  182.8 0.7 copy-start.2

commit v5 on v4

--- a/solution.py
+++ b/solution.py
@@ -18,16 +18,16 @@
 DP = ("xh", "z", "c")
 eps = 1e-05
 rope_base = 500000.0
-VMEM_LIMIT = 60 * 1024 * 1024
+VMEM_LIMIT = 59 * 1024 * 1024
 F32 = jnp.float32
 BF16 = jnp.bfloat16
 
 PIECES = 8
-EVEN_DOWN = (0, 1, 2, 3)
-ODD_DOWN = (0,)
-ODD_UP = (2, 3)
+EVEN_DOWN = (0, 1, 2)
+ODD_DOWN = (0, 2)
+ODD_UP = (1,)
 DOWN = tuple(sorted(set(EVEN_DOWN + ODD_DOWN)))
-SEND_ORDER = (0, 4, 1, 5, 2, 6, 3, 7)
+SEND_ORDER = (0, 4, 1, 5, 2, 6, 7, 3)
 KEY_ORDER = (2, 3, 0, 1)
 SUBS = 2
 
@@ -68,11 +68,12 @@
 
 def kernel(
     ny, nz,
-    x_ref, cot_ref, wk_ref, wv_ref, gain_ref, plan_ref, cos_ref, sin_ref,
+    x_in, cot_in, wk_in, wv_in, gain_in, plan_ref, cos_in, sin_in,
     low_out, key_out, value_out, gain_out,
+    x_ref, wk_ref, wv_ref, gain_ref, cos_ref, sin_ref,
     fk, fv, fg, gown, up_ref, low_s, via_ref, hill_ref, normed_s, out_rows, rows_all, key_s, value_s, query_s,
     prob_s, inv_s, drop_s, qb_s, pre_k, pre_v, kv_s, kv_all, col_s, col_all, sbuf, rbuf, gsend, grecv,
-    xs, xr, zs, zr, ws, wr, ds, dr, ls, lr, bs, br,
+    ld, xs, xr, zs, zr, ws, wr, ds, dr, ls, lr, bs, br,
     us, ur, vs, vr, fs, hs, hr, ns, nr, ks, kr, cs, cr, rs, rr, gs, gr,
 ):
     y, xl = lax.axis_index("y"), lax.axis_index("xl")
@@ -95,12 +96,28 @@
     toward = (ring[0], ring[nz - 2])
     long_way, short_way = nz // 2, nz - 1 - nz // 2
 
-    gown[...] = jnp.broadcast_to(gain_ref[...].astype(F32), gown.shape)
+    held = (
+        (gain_in, gain_ref), (wk_in, wk_ref), (wv_in, wv_ref),
+        (x_in, x_ref), (cos_in, cos_ref), (sin_in, sin_ref),
+    )
+    loads = [pltpu.make_async_copy(src, dst, ld.at[n]) for n, (src, dst) in enumerate(held)]
+    for load in loads:
+        load.start()
+    cot_load = pltpu.make_async_copy(cot_in, up_ref, ld.at[len(held)])
+
+    @pl.when(section == sections - 1)
+    def _():
+        cot_load.start()
+
     barrier = pltpu.get_barrier_semaphore()
     greeted = [across, partner, corner, below, above, two_below, two_above]
     greeted += [three_below, three_above] + ring
     for peer in greeted:
         pl.semaphore_signal(barrier, inc=1, device_id=peer, device_id_type=MESH_ID)
+    loads[0].wait()
+    gown[...] = jnp.broadcast_to(gain_ref[...].astype(F32), gown.shape)
+    loads[1].wait()
+    loads[2].wait()
     pl.semaphore_wait(barrier, len(greeted))
 
     sends = []
@@ -109,13 +126,11 @@
         copy.start()
         sends.append(copy)
 
-    cosine, sine = cos_ref[...], sin_ref[...]
-
     def rotate(v):
-        return v * cosine + pltpu.roll(v, HEAD_DIM // 2, axis=1) * sine
+        return v * cos_ref[...] + pltpu.roll(v, HEAD_DIM // 2, axis=1) * sin_ref[...]
 
     def unrotate(v):
-        return v * cosine - pltpu.roll(v, HEAD_DIM // 2, axis=1) * sine
+        return v * cos_ref[...] - pltpu.roll(v, HEAD_DIM // 2, axis=1) * sin_ref[...]
 
     def gain(h):
         return fg[h // (2 * nz), h % 2, (h // 2) % nz, 0:1, :]
@@ -212,6 +227,8 @@
     fg[xh, c, z] = gown[...]
     push(remote(sources[0], place(0, 0, 0), xs.at[0], xr.at[0], across))
     push(remote(sources[1], place(1, 0, 0), ws.at[0], wr.at[0], across))
+    for load in loads[3:]:
+        load.wait()
     mean_square(0)
     mean_square(1)
 
@@ -299,7 +316,7 @@
 
     @pl.when(section == sections - 1)
     def _():
-        up_ref[...] = cot_ref[...]
+        cot_load.wait()
 
     def piece(ref, i, j):
         return ref.at[i, :, pl.ds(j * piece_width, piece_width)]
@@ -631,11 +648,17 @@
             jax.ShapeDtypeStruct((depth, kv_width), F32),
             jax.ShapeDtypeStruct((1, depth), F32),
         ],
-        in_specs=[pl.BlockSpec(memory_space=pltpu.VMEM)] * 5
+        in_specs=[pl.BlockSpec(memory_space=pltpu.HBM)] * 5
         + [pl.BlockSpec(memory_space=pltpu.SMEM)]
-        + [pl.BlockSpec(memory_space=pltpu.VMEM)] * 2,
+        + [pl.BlockSpec(memory_space=pltpu.HBM)] * 2,
         out_specs=[pl.BlockSpec(memory_space=pltpu.VMEM)] * 4,
         scratch_shapes=[
+            pltpu.VMEM((batches, tokens, width), BF16),
+            pltpu.VMEM((depth, kv_width), BF16),
+            pltpu.VMEM((depth, kv_width), BF16),
+            pltpu.VMEM((1, depth), BF16),
+            pltpu.VMEM((tokens, HEAD_DIM), F32),
+            pltpu.VMEM((tokens, HEAD_DIM), F32),
             pltpu.VMEM((2, nz, 2, depth, kv_width), BF16),
             pltpu.VMEM((2, nz, 2, depth, kv_width), BF16),
             pltpu.VMEM((2, 2, nz, 8, depth), F32),
@@ -664,6 +687,7 @@
             pltpu.VMEM((*hop_ring, depth // SUBS, kv_width), BF16),
             pltpu.VMEM((nz, 8, HEAD_DIM), F32),
             pltpu.VMEM((nz - 1, 8, HEAD_DIM), F32),
+            dma((7,)),
             *both(1),
             *both(2, half, 2, 2),
             *both(1 + 2 * half),

time: 184 us -> 180 us (0.978)
  Pallas kernels: 179 us -> 175 us
    pallas_call x1, Pallas kernels: 179 us -> 175 us  [whole(): pl.pallas_call(functools.partial(kernel, ny, nz), out_shape=[jax.ShapeDty...]
where the time goes in v5:
time: 180 us
  Pallas kernels  175 us (97%)
  local copies, waits for them, and re-layouts  4.59 us (3%)
    pallas_call x1, Pallas kernels, whole(): pl.pallas_call(functools.partial(kernel, ny, nz), out_shape=[jax.ShapeDty...  175 us
    unnamed x10, local copies, waits for them, and re-layouts  4.59 us

profile of v5, /device:TPU:1, one launch (start us, length us, event | category | flops | bytes accessed | tf_op | source)
XLA Modules:
  0.0 180.1 jit_solution(3049018426364784100)
XLA Ops:
  0.6 174.9 %whole.1 = (bf16[2,64,4096]{2,1,0:T(8,128)(2,1)}, f32[128,512]{1,0:T(8,128)}, f32[128,512]{1,0:T(8,128)}, f32[1,128]{1,0:T(1,128)}) custom-call(bf16[2,64,4096]{2,1,0:T(8,128)(2,1)} %bitcast.6, bf16[2,64,4096]{2,1,0:T(8,128)(2,1)} %cot_in.1, bf16[128,512]{1,0:T(8,128)(2,1)} %bitcast.10, bf16[128,512]{1,0:T(8,128)(2,1)} %bitcast.11, bf16[1,128]{1,0:T(2,128)(2,1)} %gain_in.1, ...), custom_call_target="tpu_custom_call" | custom-call | tf_op jit(solution)/shard_map/whole/pallas_call | solution.py:643
  175.5 0.0 copy-start.1
  175.5 2.3 %copy.16 = bf16[1,2,64,4096]{3,2,1,0:T(8,128)(2,1)} copy(bf16[1,2,64,4096]{3,2,1,0:T(8,128)(2,1)} %bitcast.7) | data formatting | bytes 2097152
  177.8 0.0 copy-done.1
  177.8 0.0 copy-start
  177.8 0.7 copy.17
  178.5 0.3 copy-done
  178.9 0.0 copy-start.2
  178.9 0.7 copy.18
  179.6 0.0 copy-done.2
  179.6 0.5 copy.19
Async XLA Ops:
  175.5 2.3 %copy-start.1 = (f32[128,512]{1,0:T(8,128)S(1)}, f32[128,512]{1,0:T(8,128)}, u32[]{:S(2)}) copy-start(f32[128,512]{1,0:T(8,128)} %get-tuple-element.9) | copy-start | bytes 786436
  177.8 1.0 copy-start
  178.9 0.7 copy-start.2

commit v6 on v5

--- a/solution.py
+++ b/solution.py
@@ -18,7 +18,7 @@
 DP = ("xh", "z", "c")
 eps = 1e-05
 rope_base = 500000.0
-VMEM_LIMIT = 59 * 1024 * 1024
+VMEM_LIMIT = 52 * 1024 * 1024
 F32 = jnp.float32
 BF16 = jnp.bfloat16
 
@@ -68,9 +68,9 @@
 
 def kernel(
     ny, nz,
-    x_in, cot_in, wk_in, wv_in, gain_in, plan_ref, cos_in, sin_in,
+    x_in, cot_in, wk_in, wv_in, gain_in, plan_ref, tables_in,
     low_out, key_out, value_out, gain_out,
-    x_ref, wk_ref, wv_ref, gain_ref, cos_ref, sin_ref,
+    x_ref, wk_ref, wv_ref, gain_ref, tables_ref,
     fk, fv, fg, gown, up_ref, low_s, via_ref, hill_ref, normed_s, out_rows, rows_all, key_s, value_s, query_s,
     prob_s, inv_s, drop_s, qb_s, pre_k, pre_v, kv_s, kv_all, col_s, col_all, sbuf, rbuf, gsend, grecv,
     ld, xs, xr, zs, zr, ws, wr, ds, dr, ls, lr, bs, br,
@@ -98,7 +98,7 @@
 
     held = (
         (gain_in, gain_ref), (wk_in, wk_ref), (wv_in, wv_ref),
-        (x_in, x_ref), (cos_in, cos_ref), (sin_in, sin_ref),
+        (x_in, x_ref), (tables_in, tables_ref),
     )
     loads = [pltpu.make_async_copy(src, dst, ld.at[n]) for n, (src, dst) in enumerate(held)]
     for load in loads:
@@ -127,10 +127,10 @@
         sends.append(copy)
 
     def rotate(v):
-        return v * cos_ref[...] + pltpu.roll(v, HEAD_DIM // 2, axis=1) * sin_ref[...]
+        return v * tables_ref[0] + pltpu.roll(v, HEAD_DIM // 2, axis=1) * tables_ref[1]
 
     def unrotate(v):
-        return v * cos_ref[...] - pltpu.roll(v, HEAD_DIM // 2, axis=1) * sin_ref[...]
+        return v * tables_ref[0] - pltpu.roll(v, HEAD_DIM // 2, axis=1) * tables_ref[1]
 
     def gain(h):
         return fg[h // (2 * nz), h % 2, (h // 2) % nz, 0:1, :]
@@ -650,15 +650,14 @@
         ],
         in_specs=[pl.BlockSpec(memory_space=pltpu.HBM)] * 5
         + [pl.BlockSpec(memory_space=pltpu.SMEM)]
-        + [pl.BlockSpec(memory_space=pltpu.HBM)] * 2,
+        + [pl.BlockSpec(memory_space=pltpu.HBM)],
         out_specs=[pl.BlockSpec(memory_space=pltpu.VMEM)] * 4,
         scratch_shapes=[
             pltpu.VMEM((batches, tokens, width), BF16),
             pltpu.VMEM((depth, kv_width), BF16),
             pltpu.VMEM((depth, kv_width), BF16),
             pltpu.VMEM((1, depth), BF16),
-            pltpu.VMEM((tokens, HEAD_DIM), F32),
-            pltpu.VMEM((tokens, HEAD_DIM), F32),
+            pltpu.VMEM((2, tokens, HEAD_DIM), F32),
             pltpu.VMEM((2, nz, 2, depth, kv_width), BF16),
             pltpu.VMEM((2, nz, 2, depth, kv_width), BF16),
             pltpu.VMEM((2, 2, nz, 8, depth), F32),
@@ -687,7 +686,7 @@
             pltpu.VMEM((*hop_ring, depth // SUBS, kv_width), BF16),
             pltpu.VMEM((nz, 8, HEAD_DIM), F32),
             pltpu.VMEM((nz - 1, 8, HEAD_DIM), F32),
-            dma((7,)),
+            dma((6,)),
             *both(1),
             *both(2, half, 2, 2),
             *both(1 + 2 * half),
@@ -708,7 +707,7 @@
             collective_id=0, has_side_effects=True, vmem_limit_bytes=VMEM_LIMIT
         ),
         name="whole",
-    )(x, cot, wk, wv, gain, plan, jnp.asarray(cosine), jnp.asarray(sine))
+    )(x, cot, wk, wv, gain, plan, jnp.asarray(np.stack([cosine, sine])))
 
 
 def solution(mesh):

time: 180 us -> 181 us (level)
    unnamed x10 -> x14, local copies, waits for them, and re-layouts: 4.59 us -> 6.19 us
where the time goes in v6:
time: 181 us
  Pallas kernels  174 us (96%)
  local copies, waits for them, and re-layouts  6.19 us (3%)
    pallas_call x1, Pallas kernels, whole(): pl.pallas_call(functools.partial(kernel, ny, nz), out_shape=[jax.ShapeDty...  174 us
    unnamed x14, local copies, waits for them, and re-layouts  6.19 us

profile of v6, /device:TPU:1, one launch (start us, length us, event | category | flops | bytes accessed | tf_op | source)
XLA Modules:
  0.0 180.7 jit_solution(17594190223955421867)
XLA Ops:
  0.6 0.0 copy-start.3
  0.6 0.0 copy-start.4
  0.7 0.6 copy-done.3
  1.3 0.0 copy-done.4
  1.3 0.0 copy-start
  1.3 0.9 copy-done
  2.2 0.0 copy-start.1
  2.2 0.9 copy-done.1
  3.1 0.0 copy-start.2
  3.1 0.8 copy-done.2
  4.0 173.8 %whole.1 = (bf16[2,64,4096]{2,1,0:T(8,128)(2,1)S(1)}, f32[128,512]{1,0:T(8,128)S(1)}, f32[128,512]{1,0:T(8,128)S(1)}, f32[1,128]{1,0:T(1,128)S(1)}) custom-call(bf16[2,64,4096]{2,1,0:T(8,128)(2,1)} %bitcast.11, bf16[2,64,4096]{2,1,0:T(8,128)(2,1)} %cot_in.1, bf16[128,512]{1,0:T(8,128)(2,1)S(1)} %bitcast.9, bf16[128,512]{1,0:T(8,128)(2,1)S(1)} %bitcast.10, ...), custom_call_target="tpu_custom_call" | custom-call | tf_op jit(solution)/shard_map/whole/pallas_call | solution.py:643
  177.8 1.0 copy.15
  178.8 0.7 copy.16
  179.5 0.7 copy.17
  180.2 0.5 copy.18
Async XLA Ops:
  0.6 0.7 copy-start.3
  0.6 0.7 copy-start.4
  1.3 0.9 copy-start
  2.2 0.9 copy-start.1
  3.1 0.8 copy-start.2
